TPU v7x, 128 devices: a whole 4x4x4 slice. The times are simulated.
128 devices in a mesh: row: 16 (over y, x_lo, core), col: 8 (over x_hi, z).
Axes of the slice: x: 4 (x_hi: 2, x_lo: 2; x = x_hi * 2 + x_lo), y: 4, z: 4, core: 2. Of those that a mesh axis runs over, the one named last changes fastest.
Arguments:
- adjacency: int32 [10240, 320], P('row', 'col'), may hold values from -2147483648 to 2147483647, as said below
- relabel: int32 [10240], P(('row', 'col')), may hold values from 0 to 10239, each once
Outputs:
- clustering: float32 [10240], P(('row', 'col'))
- transitivity: float32 [], replicated
Inputs may be any that keep to these rules, and one draw needn't show every extreme that they name: The unpacked adjacency is symmetric with a zero diagonal.
All inputs are finite; a program needn't handle non-finite values.
Results may differ from a plain program's by a relative error of at most 0.0003.
Values sent between devices are 32-bit elements.
No kernel may reach another device: no remote copies, remote signals or barrier semaphores. Data moves between devices by JAX's collectives and lax.ppermute only.
A program may use at most 128 MiB of HBM per device.

v0:
```python
import jax
import jax.numpy as jnp
from jax import lax
from jax.sharding import PartitionSpec as P


def sent_to_all(value, axis):
    peers = lax.axis_size(axis)
    return lax.all_to_all(
        jnp.broadcast_to(value[None], (peers, *value.shape)), axis, 0, 0, tiled=True
    )


def laid_out(tiles, dim):
    tiles = jnp.moveaxis(tiles, 0, dim)
    dims = tiles.shape
    return tiles.reshape(*dims[:dim], dims[dim] * dims[dim + 1], *dims[dim + 2 :])


def gathered_copies(value, axis, dim):
    tiles = sent_to_all(value, axis)
    return laid_out(tiles, dim)


def cut_along(value, dim, peers):
    before, after = (value.shape[:dim], value.shape[dim + 1 :])
    return jnp.moveaxis(value.reshape(*before, peers, -1, *after), dim, 0)


def summed_on_arrival(value, axis, dim):
    tiles = cut_along(value, dim, lax.axis_size(axis))
    arrived = lax.all_to_all(tiles, axis, split_axis=0, concat_axis=0, tiled=True)
    return arrived.sum(axis=0)


def over_pieces(value, axis):
    return lax.all_gather(value, axis).sum(0)


def unpack(words):
    shifts = jnp.arange(32, dtype=jnp.int32)
    bits = lax.shift_right_logical(words[:, :, None], shifts[None, None, :]) & 1
    return bits.reshape(words.shape[0], words.shape[1] * 32).astype(jnp.bfloat16)


def body(adjacency, relabel):
    local = unpack(adjacency)
    row_block = unpack(gathered_copies(adjacency, "col", 1))
    paths = jnp.dot(
        row_block,
        unpack(lax.all_gather(adjacency, "row", axis=0, tiled=True)),
        preferred_element_type=jnp.float32,
    )
    wide = local.astype(jnp.float32)
    partial_value = jnp.sum(wide * paths, axis=1)
    degree_part = jnp.sum(wide, axis=1)
    closed, degree = (
        summed_on_arrival(partial_value, "col", 0),
        summed_on_arrival(degree_part, "col", 0),
    )
    wedges = jnp.maximum(degree * (degree - 1.0), 1.0)
    everyone = lax.all_gather(closed / wedges, ("row", "col"), axis=0, tiled=True)
    clustering = jnp.take(everyone, relabel, axis=0)
    sum_closed, sum_wedges = (
        over_pieces(jnp.sum(closed), ("row", "col")),
        over_pieces(jnp.sum(wedges), ("row", "col")),
    )
    transitivity = sum_closed / sum_wedges
    return (clustering, transitivity)


def solution(mesh):
    placed = (P("row", "col"), P(("row", "col")))
    return jax.shard_map(
        body, mesh=mesh, in_specs=placed, out_specs=(P(("row", "col")), P()), check_vma=False
    )
```

profile of v0, /device:TPU:1, one launch (start us, length us, event | category | flops | bytes accessed | tf_op | source)
XLA Modules:
  0.0 179.7 jit_solution(8041186109363718358)
XLA Ops:
  7.2 0.0 all-gather.2.cloned.1.call-start
  7.2 0.7 all-gather.2.cloned.1.call-update
  7.9 1.9 %broadcast_in_dim.8 = s32[8,640,40]{1,2,0:T(8,128)} broadcast(s32[640,40]{0,1:T(8,128)} %param.2), dimensions={1,2} | broadcast | bytes 921600 | tf_op jit(solution)/shard_map/broadcast_in_dim | solution.py:10
  9.7 8.3 %all-to-all-start = ((s32[8,640,40]{1,2,0:T(8,128)}), s32[8,640,40]{1,2,0:T(8,128)}, u32[]{:S(2)}, u32[]{:S(2)}) async-start(s32[8,640,40]{1,2,0:T(8,128)} %broadcast_in_dim.8), calls=%async_computation | async-start | bytes 1638400 | tf_op jit(solution)/shard_map/all_to_all | solution.py:9
  18.1 1.4 convert_reduce_fusion
  19.5 0.7 all_to_all.18
  20.2 0.1 shift_right_logical.72
  20.3 1.1 shift_right_logical.69
  21.4 3.0 %copy.9 = s32[640,1280]{1,0:T(8,128)} copy(s32[640,1280]{0,1:T(8,128)S(1)} %bitcast.14) | data formatting | bytes 6553600 | tf_op jit(solution)/shard_map/shift_right_logical | solution.py:42
  24.4 0.7 compare_select_fusion
  25.0 7.4 %all-to-all-done = s32[8,640,40]{1,2,0:T(8,128)} async-done(((s32[8,640,40]{1,2,0:T(8,128)}), s32[8,640,40]{1,2,0:T(8,128)}, u32[]{:S(2)}, u32[]{:S(2)}) %all-to-all-start) | async-done | bytes 819232 | tf_op jit(solution)/shard_map/all_to_all | solution.py:9
  32.4 3.9 %all-to-all-start.2 = ((f32[8,1,80]{2,1,0:T(1,128)}), f32[8,1,80]{2,1,0:T(1,128)S(1)}, u32[]{:S(2)}, u32[]{:S(2)}) async-start(f32[8,1,80]{2,1,0:T(1,128)} %all_to_all.18), calls=%async_computation.2 | async-start | bytes 8192 | tf_op jit(solution)/shard_map/all_to_all | solution.py:32
  36.3 10.3 %and_convert_fusion.1 = bf16[640,320,32]{0,2,1:T(8,128)(2,1)} fusion(s32[640,320]{0,1:T(8,128)} %bitcast.2), kind=kLoop, calls=%fused_computation.2 | loop fusion | flops 19660800 | bytes 13926400 | tf_op jit(solution)/shard_map/convert_element_type | solution.py:43
  46.6 0.8 all-gather.2.cloned.1.call-done
  47.5 0.0 copy-start
  47.5 14.2 %and_convert_fusion = bf16[10240,40,32]{0,2,1:T(8,128)(2,1)} fusion(s32[10240,40]{0,1:T(8,128)} %all-gather.2.cloned.1.call-done), kind=kLoop, calls=%fused_computation.1 | loop fusion | flops 39321600 | bytes 27852800 | tf_op jit(solution)/shard_map/convert_element_type | solution.py:43
  61.7 0.0 copy-done
  61.7 21.8 %fusion = f32[640]{0:T(1024)S(1)} fusion(bf16[640,10240]{0,1:T(8,128)(2,1)S(1)} %bitcast.15, bf16[10240,1280]{0,1:T(8,128)(2,1)} %bitcast.13, s32[640,1280]{1,0:T(8,128)} %copy.9, s32[1280]{0:T(1024)S(1)} %shift_right_logical.72), kind=kOutput, calls=%fused_computation.7 | convolution fusion | flops 16782130176 | bytes 42606080 | tf_op jit(solution)/shard_map/dot_general | solution.py:49
  83.4 0.7 all_to_all.16
  84.1 0.0 all-to-all-done.2
  84.1 6.1 %all-to-all-start.1 = ((f32[8,1,80]{2,1,0:T(1,128)}), f32[8,1,80]{2,1,0:T(1,128)S(1)}, u32[]{:S(2)}, u32[]{:S(2)}) async-start(f32[8,1,80]{2,1,0:T(1,128)} %all_to_all.16), calls=%async_computation.1 | async-start | bytes 8192 | tf_op jit(solution)/shard_map/all_to_all | solution.py:32
  90.3 6.5 %all-to-all-done.1 = f32[8,1,80]{2,1,0:T(1,128)S(1)} async-done(((f32[8,1,80]{2,1,0:T(1,128)}), f32[8,1,80]{2,1,0:T(1,128)S(1)}, u32[]{:S(2)}, u32[]{:S(2)}) %all-to-all-start.1) | async-done | bytes 2592 | tf_op jit(solution)/shard_map/all_to_all | solution.py:32
  96.8 0.6 fusion.3
  97.4 0.7 fusion.2
  98.1 0.8 dynamic-update-slice.2
  98.8 0.8 dynamic-update-slice.1
  99.6 67.8 %all-reduce.3 = (f32[10240]{0:T(1024)S(1)}, f32[128]{0:T(128)S(1)}, f32[128]{0:T(128)S(1)}) all-reduce(f32[10240]{0:T(1024)S(1)} %get-tuple-element.8, f32[128]{0:T(128)S(1)} %dynamic-update-slice.1, f32[128]{0:T(128)S(1)} %dynamic-update-slice.2), channel_id=1, replica_groups=mesh['row'=16,'col'=8] {'row','col'}, use_global_device_ids=true, to_apply=%add | all-reduce | flops 10496 | bytes 83968
  167.4 1.1 gather_fusion
  168.5 0.0 copy-done.1
  168.5 0.5 and_select_fusion
  169.0 0.7 reduce_sum.79
  169.7 0.6 reduce_sum.77
  (7 shorter events, 0.0 us)
Async XLA Ops:
  7.2 40.3 %all-gather.2.cloned.1.call-start = ((), (), s32[]{:S(2)}) async-start(), calls=%async_computation.3 | async-start | bytes 1740800 | tf_op jit(solution)/shard_map/all_gather | solution.py:51
  9.7 22.7 %all-to-all-start = ((s32[8,640,40]{1,2,0:T(8,128)}), s32[8,640,40]{1,2,0:T(8,128)}, u32[]{:S(2)}, u32[]{:S(2)}) async-start(s32[8,640,40]{1,2,0:T(8,128)} %broadcast_in_dim.8), calls=%async_computation | async-start | bytes 1638400 | tf_op jit(solution)/shard_map/all_to_all | solution.py:9
  32.4 51.7 %all-to-all-start.2 = ((f32[8,1,80]{2,1,0:T(1,128)}), f32[8,1,80]{2,1,0:T(1,128)S(1)}, u32[]{:S(2)}, u32[]{:S(2)}) async-start(f32[8,1,80]{2,1,0:T(1,128)} %all_to_all.18), calls=%async_computation.2 | async-start | bytes 8192 | tf_op jit(solution)/shard_map/all_to_all | solution.py:32
  47.5 14.2 %copy-start = (bf16[640,320,32]{0,2,1:T(8,128)(2,1)S(1)}, bf16[640,320,32]{0,2,1:T(8,128)(2,1)}, u32[]{:S(2)}) copy-start(bf16[640,320,32]{0,2,1:T(8,128)(2,1)} %and_convert_fusion.1) | copy-start | bytes 39321604
  61.7 106.8 %copy-start.1 = (s32[80]{0:T(128)S(1)}, s32[80]{0:T(128)}, u32[]{:S(2)}) copy-start(s32[80]{0:T(128)} %param.3) | copy-start | bytes 964
  84.1 12.7 %all-to-all-start.1 = ((f32[8,1,80]{2,1,0:T(1,128)}), f32[8,1,80]{2,1,0:T(1,128)S(1)}, u32[]{:S(2)}, u32[]{:S(2)}) async-start(f32[8,1,80]{2,1,0:T(1,128)} %all_to_all.16), calls=%async_computation.1 | async-start | bytes 8192 | tf_op jit(solution)/shard_map/all_to_all | solution.py:32
Sparse Core Ops, SparseCore 0:
  9.6 37.8 all-gather.1
where the time goes:
time: 180 us
  blocking collectives  67.8 us (38%)
  other arithmetic  29.7 us (16%)
  matrix products  21.8 us (12%)
  starting transfers between devices  18.3 us (10%)
  between operations  16.6 us (9%)
  waiting for transfers between devices  15.4 us (9%)
  local copies, waits for them, and re-layouts  10.1 us (6%)
    unnamed x1, blocking collectives  67.8 us
    convert_element_type x2, other arithmetic, unpack(): bits.reshape(words.shape[0], words.shape[1] * 32).astype(jnp.bfloat16)  24.5 us
    dot_general x1, matrix products, body(): jnp.dot(row_block, unpack(lax.all_gather(adjacency, 'row', axis=0, tiled=...  21.8 us
    all_to_all x2, starting transfers between devices, summed_on_arrival(): lax.all_to_all(tiles, axis, split_axis=0, concat_axis=0, tiled=True)  9.99 us
    all_to_all x1, starting transfers between devices, sent_to_all(): lax.all_to_all(jnp.broadcast_to(value[None], (peers, *value.shape)), axis...  8.31 us
    all_to_all x1, waiting for transfers between devices, sent_to_all(): lax.all_to_all(jnp.broadcast_to(value[None], (peers, *value.shape)), axis...  7.4 us
    all_to_all x2, waiting for transfers between devices, summed_on_arrival(): lax.all_to_all(tiles, axis, split_axis=0, concat_axis=0, tiled=True)  6.5 us
    shift_right_logical x4, local copies, waits for them, and re-layouts, unpack(): bits = lax.shift_right_logical(words[:, :, None], shifts[None, None, :]) & 1  4.2 us
  transfers between devices with their start and end apart: 4, of which 3 were waited for; matrix products, arithmetic and copies ran while one was open for 30% of the time, Pallas kernels for 0%

commit v1 on v0

v1 whole, which is shorter than its diff:
```python
import jax
import jax.numpy as jnp
from jax import lax
from jax.experimental import pallas as pl
from jax.experimental.pallas import tpu as pltpu
from jax.sharding import PartitionSpec as P

ALL = ("row", "col")
WINDOW = 5
WEIGHTS = (1.0, 2.0, 2.0, 2.0, 1.0)


def spread(value, peers):
    return jnp.broadcast_to(value[None], (peers, *value.shape))


def unpacked(row, value, dtype):
    lanes = row.shape[1]
    bit = lax.broadcasted_iota(jnp.int32, (32, lanes), 0)
    hit = (row & lax.shift_left(jnp.int32(1), bit)) != 0
    return jnp.where(hit, jnp.float32(value), jnp.float32(0)).astype(dtype)


def count_kernel(own, oth, r0, r1, r2, r3, r4, out, rhs, lhs, acc, *, dtype):
    core = lax.rem(lax.axis_index("row"), 2)
    col = lax.axis_index("col")
    words, lanes = r0.shape
    half = words // 2
    depth = words * 32
    rows = (r0, r1, r2, r3, r4)
    for t in range(WINDOW):

        def fill_rhs(w, _, t=t):
            src = lax.rem(core * half + w, words)
            at = pl.multiple_of(t * depth + w * 32, 32)
            rhs[pl.ds(at, 32), :] = unpacked(rows[t][pl.ds(src, 1), :], WEIGHTS[t], dtype)
            return 0

        lax.fori_loop(0, words, fill_rhs, 0)

    acc[...] = jnp.zeros_like(acc)

    def step(t, _):
        block = lax.rem(col + t, 8)

        def fill_lhs(w, _):
            at = pl.multiple_of(w * 32, 32)
            lhs[pl.ds(at, 32), :lanes] = unpacked(own[block, pl.ds(w, 1), :], 1.0, dtype)
            lhs[pl.ds(at, 32), lanes:] = unpacked(oth[block, pl.ds(w, 1), :], 1.0, dtype)
            return 0

        lax.fori_loop(0, words, fill_lhs, 0)
        at = pl.multiple_of(t * depth, depth)
        acc[...] += jnp.dot(
            lhs[...], rhs[pl.ds(at, depth), :], preferred_element_type=jnp.float32
        )
        return 0

    lax.fori_loop(0, WINDOW, step, 0)

    def masked(w, total):
        at = pl.multiple_of(w * 32, 32)
        bit = lax.broadcasted_iota(jnp.int32, (32, lanes), 0)
        hit = (r0[pl.ds(w, 1), :] & lax.shift_left(jnp.int32(1), bit)) != 0
        picked = jnp.where(hit, acc[pl.ds(at, 32), :], 0.0)
        return total + picked.reshape(4, 8, lanes).sum(axis=0)

    total = lax.fori_loop(0, words, masked, jnp.zeros((8, lanes), jnp.float32))
    closed = jnp.sum(total, axis=0, keepdims=True)
    links = sum(lax.population_count(rows[t][...]) for t in range(4))
    degree = jnp.sum(links, axis=0, keepdims=True).astype(jnp.float32)
    degree = jnp.concatenate([degree, jnp.zeros((1, 128), jnp.float32)], axis=1)
    part = lax.rem(col, 4)
    window = jnp.where(
        part == 0, degree[:, :256], jnp.where(part == 1, degree[:, 256:512], degree[:, 512:768])
    )
    payload = jnp.concatenate([closed, window], axis=1)
    out[...] = jnp.broadcast_to(payload, out.shape)


def finish_kernel(parts, relabel, clustering, transitivity):
    value = parts[...].reshape(16, 8, 896)
    closed = value[:, :, :640].sum(axis=1)
    slot = lax.rem(lax.broadcasted_iota(jnp.int32, (16, 8, 256), 1), 4)
    window = value[:, :, 640:]
    pieces = [jnp.where(slot == m, window, 0.0).sum(axis=1) for m in range(3)]
    degree = jnp.concatenate([pieces[0], pieces[1], pieces[2][:, :128]], axis=1)
    wedges = jnp.maximum(degree * (degree - 1.0), 1.0)
    ratio = closed / wedges
    index = relabel[...]
    block = index // 640
    lane = index - block * 640
    hot = (lax.broadcasted_iota(jnp.int32, (640, 80), 0) == lane).astype(jnp.float32)
    picked = jnp.dot(
        ratio, hot, preferred_element_type=jnp.float32, precision=lax.Precision.HIGHEST
    )
    mine = lax.broadcasted_iota(jnp.int32, (16, 80), 0) == block
    clustering[...] = jnp.sum(jnp.where(mine, picked, 0.0), axis=0, keepdims=True)
    total = jnp.sum(jnp.sum(closed, axis=0, keepdims=True), axis=1, keepdims=True)
    pairs = jnp.sum(jnp.sum(wedges, axis=0, keepdims=True), axis=1, keepdims=True)
    transitivity[...] = total / pairs


def body(adjacency, relabel, dtype=jnp.bfloat16):
    words = adjacency.T
    rows = [words] + [
        lax.ppermute(words, "col", [((c + t) % 8, c) for c in range(8)])
        for t in range(1, WINDOW)
    ]
    cores = [[2 * chip + core for chip in range(8)] for core in range(2)]
    own = lax.all_to_all(
        spread(words, 8), "row", 0, 0, axis_index_groups=cores, tiled=True
    )
    oth = lax.ppermute(own, "row", [(r, r ^ 1) for r in range(16)])
    vmem = pl.BlockSpec(memory_space=pltpu.VMEM)
    depth = words.shape[0] * 32
    lanes = words.shape[1]

    def kernel(*refs):
        count_kernel(*refs, dtype=dtype)

    payload = pl.pallas_call(
        kernel,
        out_shape=jax.ShapeDtypeStruct((128, 896), jnp.float32),
        in_specs=[vmem] * 7,
        out_specs=vmem,
        scratch_shapes=[
            pltpu.VMEM((WINDOW * depth, lanes), dtype),
            pltpu.VMEM((depth, depth), dtype),
            pltpu.VMEM((depth, lanes), jnp.float32),
        ],
        compiler_params=pltpu.CompilerParams(vmem_limit_bytes=60 * 2**20),
        name="count",
    )(own, oth, *rows)
    parts = lax.all_to_all(payload, ALL, 0, 0, tiled=True)
    clustering, transitivity = pl.pallas_call(
        finish_kernel,
        out_shape=(
            jax.ShapeDtypeStruct((1, 80), jnp.float32),
            jax.ShapeDtypeStruct((1, 1), jnp.float32),
        ),
        in_specs=[vmem] * 2,
        out_specs=(vmem, vmem),
        name="finish",
    )(parts, relabel[None])
    return clustering[0], transitivity[0, 0]


def solution(mesh):
    return jax.shard_map(
        body,
        mesh=mesh,
        in_specs=(P("row", "col"), P(ALL)),
        out_specs=(P(ALL), P()),
        check_vma=False,
    )
```

time: 180 us -> 91.2 us (0.51)
  blocking collectives: 67.8 us -> 37.9 us
  other arithmetic: 29.7 us -> 0 us
  Pallas kernels: 0 us -> 29.5 us
  matrix products: 21.8 us -> 0 us
  between operations: 16.6 us -> 0.68 us
  waiting for transfers between devices: 15.4 us -> 5.29 us
  starting transfers between devices: 18.3 us -> 12.7 us
  local copies, waits for them, and re-layouts: 10.1 us -> 4.8 us
    unnamed x1 -> x0, blocking collectives: 67.8 us -> none
    all_to_all x0 -> x2, blocking collectives: none -> 37.9 us  [the longest x1 19.8 us: body(): parts = lax.all_to_all(payload, ALL, 0, 0, tiled=True)]
    pallas_call x0 -> x2, Pallas kernels: none -> 29.5 us  [the longest x1 27.5 us: body(): pl.pallas_call(kernel, out_shape=jax.ShapeDtypeStruct((128, 896), jnp.flo...]
    convert_element_type x2 -> x0, other arithmetic: 24.5 us -> none  [unpack(): bits.reshape(words.shape[0], words.shape[1] * 32).astype(jnp.bfloat16)]
    dot_general x1 -> x0, matrix products: 21.8 us -> none  [body(): jnp.dot(row_block, unpack(lax.all_gather(adjacency, 'row', axis=0, tiled=...]
    all_to_all x3 -> x0, starting transfers between devices: 18.3 us -> none  [the longest x2 9.99 us: summed_on_arrival(): lax.all_to_all(tiles, axis, split_axis=0, concat_axis=0, tiled=True)]
    all_to_all x3 -> x0, waiting for transfers between devices: 13.9 us -> none  [the longest x1 7.4 us: sent_to_all(): lax.all_to_all(jnp.broadcast_to(value[None], (peers, *value.shape)), axis...]
    ppermute x0 -> x5, starting transfers between devices: none -> 12.7 us  [the longest x4 10.5 us: body(): lax.ppermute(words, 'col', [((c + t) % 8, c) for c in range(8)])]
  transfers between devices with their start and end apart: 4 -> 5, of which waited for: 3 -> 3; matrix products, arithmetic and copies ran while one was open for 30% -> 0% of each run, Pallas kernels for 0% -> 0%
where the time goes in v1:
time: 91.2 us; the launch traced here: 90.9 us
  blocking collectives  37.9 us (42%)
  Pallas kernels  29.5 us (32%)
  starting transfers between devices  12.7 us (14%)
  waiting for transfers between devices  5.29 us (6%)
  local copies, waits for them, and re-layouts  4.8 us (5%)
    pallas_call x1, Pallas kernels, body(): pl.pallas_call(kernel, out_shape=jax.ShapeDtypeStruct((128, 896), jnp.flo...  27.5 us
    all_to_all x1, blocking collectives, body(): parts = lax.all_to_all(payload, ALL, 0, 0, tiled=True)  19.8 us
    all_to_all x1, blocking collectives, body(): lax.all_to_all(spread(words, 8), 'row', 0, 0, axis_index_groups=cores, ti...  18.1 us
    ppermute x4, starting transfers between devices, body(): lax.ppermute(words, 'col', [((c + t) % 8, c) for c in range(8)])  10.5 us
    ppermute x4, waiting for transfers between devices, body(): lax.ppermute(words, 'col', [((c + t) % 8, c) for c in range(8)])  5.29 us
    unnamed x15, local copies, waits for them, and re-layouts  2.36 us
    ppermute x1, starting transfers between devices, body(): oth = lax.ppermute(own, 'row', [(r, r ^ 1) for r in range(16)])  2.19 us
    pallas_call x1, Pallas kernels, body(): pl.pallas_call(finish_kernel, out_shape=(jax.ShapeDtypeStruct((1, 80), jn...  2.02 us
  transfers between devices with their start and end apart: 5, of which 3 were waited for; matrix products, arithmetic and copies ran while one was open for 0% of the time, Pallas kernels for 0%

profile of v1, /device:TPU:1, one launch (start us, length us, event | category | flops | bytes accessed | tf_op | source)
XLA Modules:
  0.0 90.9 jit_solution(16961473132073636403)
XLA Ops:
  0.6 0.9 %broadcast_in_dim.4 = s32[8,40,640]{2,1,0:T(8,128)S(1)} broadcast(s32[40,640]{1,0:T(8,128)} %bitcast.10), dimensions={1,2} | broadcast | bytes 921600 | tf_op jit(solution)/shard_map/broadcast_in_dim | solution.py:14
  1.6 0.0 copy-start.2
  1.6 18.1 %all_to_all.16.refs_0_ = s32[8,40,640]{2,1,0:T(8,128)S(1)} all-to-all(s32[8,40,640]{2,1,0:T(8,128)S(1)} %broadcast_in_dim.4), channel_id=1, replica_groups={{0,16,32,48,64,80,96,112},{8,24,40,56,72,88,104,120},{1,17,33,49,65,81,..., dimensions={0} | all-to-all | bytes 1638400 | tf_op jit(solution)/shard_map/all_to_all | solution.py:111
  19.7 0.0 copy-start
  19.7 2.2 %collective-permute-start = (s32[8,40,640]{2,1,0:T(8,128)S(1)}, s32[8,40,640]{2,1,0:T(8,128)S(1)}, u32[]{:S(2)}, u32[]{:S(2)}) collective-permute-start(s32[8,40,640]{2,1,0:T(8,128)S(1)} %all_to_all.16.refs_0_), channel_id=1, source_target_pairs={{0,8},{8,0},{16,24},{24,16},{32,40},{40,32},{48,56},{56,48},{64,72... | collective-permute-start | bytes 2457608 | tf_op jit(solution)/shard_map/ppermute | solution.py:114
  21.9 0.0 copy-done.2
  21.9 2.5 %collective-permute-start.4 = (s32[40,640]{1,0:T(8,128)S(1)}, s32[40,640]{1,0:T(8,128)S(1)}, u32[]{:S(2)}, u32[]{:S(2)}) collective-permute-start(s32[40,640]{1,0:T(8,128)S(1)} %bitcast.12), channel_id=1, source_target_pairs={{4,0},{5,1},{6,2},{7,3},{0,4},{1,5},{2,6},{3,7},{12,8},{13,9},{14,... | collective-permute-start | bytes 307208 | tf_op jit(solution)/shard_map/ppermute | solution.py:107
  24.3 1.9 %collective-permute-start.3 = (s32[40,640]{1,0:T(8,128)S(1)}, s32[40,640]{1,0:T(8,128)S(1)}, u32[]{:S(2)}, u32[]{:S(2)}) collective-permute-start(s32[40,640]{1,0:T(8,128)S(1)} %bitcast.13), channel_id=1, source_target_pairs={{3,0},{4,1},{5,2},{6,3},{7,4},{0,5},{1,6},{2,7},{11,8},{12,9},{13,... | collective-permute-start | bytes 307208 | tf_op jit(solution)/shard_map/ppermute | solution.py:107
  26.2 5.5 %collective-permute-start.2 = (s32[40,640]{1,0:T(8,128)S(1)}, s32[40,640]{1,0:T(8,128)S(1)}, u32[]{:S(2)}, u32[]{:S(2)}) collective-permute-start(s32[40,640]{1,0:T(8,128)S(1)} %bitcast.14), channel_id=1, source_target_pairs={{2,0},{3,1},{4,2},{5,3},{6,4},{7,5},{0,6},{1,7},{10,8},{11,9},{12,... | collective-permute-start | bytes 307208 | tf_op jit(solution)/shard_map/ppermute | solution.py:107
  31.7 0.7 collective-permute-start.1
  32.4 0.0 collective-permute-done.4.refs_6_
  32.4 0.0 copy-start.3
  32.4 0.8 collective-permute-done.3.refs_5_
  33.2 0.0 copy-start.4
  33.2 0.2 collective-permute-done.2.refs_4_
  33.3 0.0 copy-start.5
  33.3 4.3 %collective-permute-done.1.refs_3_ = s32[40,640]{1,0:T(8,128)S(1)} collective-permute-done((s32[40,640]{1,0:T(8,128)S(1)}, s32[40,640]{1,0:T(8,128)S(1)}, u32[]{:S(2)}, u32[]{:S(2)}) %collective-permute-start.1) | collective-permute-done | bytes 102432 | tf_op jit(solution)/shard_map/ppermute | solution.py:107
  37.7 0.0 copy-start.6
  37.7 0.0 collective-permute-done.refs_1_
  37.7 0.0 copy-done
  37.7 0.0 copy-done.3
  37.7 0.0 copy-done.4
  37.7 0.0 copy-done.5
  37.7 0.6 copy-done.6
  38.3 0.0 copy-start.1
  38.3 0.9 %copy-done.1 = s32[8,40,640]{2,1,0:T(8,128)} copy-done((s32[8,40,640]{2,1,0:T(8,128)}, s32[8,40,640]{2,1,0:T(8,128)S(1)}, u32[]{:S(2)}) %copy-start.1) | copy-done | bytes 819224
  39.3 27.5 %count.1 = f32[128,896]{1,0:T(8,128)} custom-call(s32[8,40,640]{2,1,0:T(8,128)} %copy-done, s32[8,40,640]{2,1,0:T(8,128)} %copy-done.1, s32[40,640]{1,0:T(8,128)} %bitcast.11, s32[40,640]{1,0:T(8,128)} %copy-done.6, s32[40,640]{1,0:T(8,128)} %copy-done.5, s32[40,640]{1,0:T(8,128)} %copy-done.4, s32[40,640]{1,0:T(8,128)} %copy-done.3), custom_call_target="tpu_custom_call" | custom-call | tf_op jit(solution)/shard_map/count/pallas_call | solution.py:122
  66.8 1.5 %copy.4 = f32[128,1,896]{2,1,0:T(1,128)S(1)} copy(f32[128,1,896]{2,0,1:T(8,128)} %bitcast.8) | data formatting | bytes 917504 | tf_op jit(solution)/shard_map/all_to_all | solution.py:135
  68.3 19.8 %all_to_all.17 = f32[128,1,896]{2,1,0:T(1,128)S(1)} all-to-all(f32[128,1,896]{2,1,0:T(1,128)S(1)} %copy.4), channel_id=1, replica_groups=mesh['row'=16,'col'=8] {'row','col'}, dimensions={0} | all-to-all | bytes 917504 | tf_op jit(solution)/shard_map/all_to_all | solution.py:135
  88.0 0.8 copy.7
  88.9 2.0 %finish.1 = (f32[1,80]{1,0:T(1,128)}, f32[1,1]{1,0:T(1,128)}) custom-call(f32[128,896]{1,0:T(8,128)} %bitcast.9, s32[1,80]{1,0:T(1,128)} %bitcast.16), custom_call_target="tpu_custom_call" | custom-call | tf_op jit(solution)/shard_map/finish/pallas_call | solution.py:136
Async XLA Ops:
  1.6 20.3 %copy-start.2 = (s32[640,40]{0,1:T(8,128)S(1)}, s32[640,40]{0,1:T(8,128)}, u32[]{:S(2)}) copy-start(s32[640,40]{0,1:T(8,128)} %param.2) | copy-start | bytes 307204
  19.7 18.0 %copy-start = (s32[8,40,640]{2,1,0:T(8,128)}, s32[8,40,640]{2,1,0:T(8,128)S(1)}, u32[]{:S(2)}) copy-start(s32[8,40,640]{2,1,0:T(8,128)S(1)} %all_to_all.16.refs_0_) | copy-start | bytes 2457604
  19.7 18.0 %collective-permute-start = (s32[8,40,640]{2,1,0:T(8,128)S(1)}, s32[8,40,640]{2,1,0:T(8,128)S(1)}, u32[]{:S(2)}, u32[]{:S(2)}) collective-permute-start(s32[8,40,640]{2,1,0:T(8,128)S(1)} %all_to_all.16.refs_0_), channel_id=1, source_target_pairs={{0,8},{8,0},{16,24},{24,16},{32,40},{40,32},{48,56},{56,48},{64,72... | collective-permute-start | bytes 2457608 | tf_op jit(solution)/shard_map/ppermute | solution.py:114
  21.9 10.5 %collective-permute-start.4 = (s32[40,640]{1,0:T(8,128)S(1)}, s32[40,640]{1,0:T(8,128)S(1)}, u32[]{:S(2)}, u32[]{:S(2)}) collective-permute-start(s32[40,640]{1,0:T(8,128)S(1)} %bitcast.12), channel_id=1, source_target_pairs={{4,0},{5,1},{6,2},{7,3},{0,4},{1,5},{2,6},{3,7},{12,8},{13,9},{14,... | collective-permute-start | bytes 307208 | tf_op jit(solution)/shard_map/ppermute | solution.py:107
  24.3 8.8 %collective-permute-start.3 = (s32[40,640]{1,0:T(8,128)S(1)}, s32[40,640]{1,0:T(8,128)S(1)}, u32[]{:S(2)}, u32[]{:S(2)}) collective-permute-start(s32[40,640]{1,0:T(8,128)S(1)} %bitcast.13), channel_id=1, source_target_pairs={{3,0},{4,1},{5,2},{6,3},{7,4},{0,5},{1,6},{2,7},{11,8},{12,9},{13,... | collective-permute-start | bytes 307208 | tf_op jit(solution)/shard_map/ppermute | solution.py:107
  26.2 7.1 %collective-permute-start.2 = (s32[40,640]{1,0:T(8,128)S(1)}, s32[40,640]{1,0:T(8,128)S(1)}, u32[]{:S(2)}, u32[]{:S(2)}) collective-permute-start(s32[40,640]{1,0:T(8,128)S(1)} %bitcast.14), channel_id=1, source_target_pairs={{2,0},{3,1},{4,2},{5,3},{6,4},{7,5},{0,6},{1,7},{10,8},{11,9},{12,... | collective-permute-start | bytes 307208 | tf_op jit(solution)/shard_map/ppermute | solution.py:107
  31.7 6.0 %collective-permute-start.1 = (s32[40,640]{1,0:T(8,128)S(1)}, s32[40,640]{1,0:T(8,128)S(1)}, u32[]{:S(2)}, u32[]{:S(2)}) collective-permute-start(s32[40,640]{1,0:T(8,128)S(1)} %bitcast.15), channel_id=1, source_target_pairs={{1,0},{2,1},{3,2},{4,3},{5,4},{6,5},{7,6},{0,7},{9,8},{10,9},{11,1... | collective-permute-start | bytes 307208 | tf_op jit(solution)/shard_map/ppermute | solution.py:107
  32.4 5.3 %copy-start.3 = (s32[40,640]{1,0:T(8,128)}, s32[40,640]{1,0:T(8,128)S(1)}, u32[]{:S(2)}) copy-start(s32[40,640]{1,0:T(8,128)S(1)} %collective-permute-done.4.refs_6_) | copy-start | bytes 307204
  33.2 4.6 %copy-start.4 = (s32[40,640]{1,0:T(8,128)}, s32[40,640]{1,0:T(8,128)S(1)}, u32[]{:S(2)}) copy-start(s32[40,640]{1,0:T(8,128)S(1)} %collective-permute-done.3.refs_5_) | copy-start | bytes 307204
  33.3 4.4 %copy-start.5 = (s32[40,640]{1,0:T(8,128)}, s32[40,640]{1,0:T(8,128)S(1)}, u32[]{:S(2)}) copy-start(s32[40,640]{1,0:T(8,128)S(1)} %collective-permute-done.2.refs_4_) | copy-start | bytes 307204
  37.7 0.6 copy-start.6
  38.3 0.9 %copy-start.1 = (s32[8,40,640]{2,1,0:T(8,128)}, s32[8,40,640]{2,1,0:T(8,128)S(1)}, u32[]{:S(2)}) copy-start(s32[8,40,640]{2,1,0:T(8,128)S(1)} %collective-permute-done.refs_1_) | copy-start | bytes 2457604

commit v2 on v1

v2 whole, which is shorter than its diff:
```python
import jax
import jax.numpy as jnp
from jax import lax
from jax.experimental import pallas as pl
from jax.experimental.pallas import tpu as pltpu
from jax.sharding import PartitionSpec as P

ALL = ("row", "col")
WINDOW = 5


def spread(value, peers):
    return jnp.broadcast_to(value[None], (peers, *value.shape))


def shifted(row, step):
    words = jnp.broadcast_to(row, (32, row.shape[1]))
    return lax.shift_right_logical(words, step)


def zero_one(row, dtype):
    bit = lax.broadcasted_iota(jnp.int32, (32, row.shape[1]), 0)
    value = (shifted(row, bit) & 1).astype(jnp.int8)
    return value.astype(jnp.bfloat16).astype(dtype)


def scaled_bits(row, dtype):
    bit = lax.broadcasted_iota(jnp.int32, (32, row.shape[1]), 0)
    octet = shifted(row, (bit // 8) * 8).astype(jnp.int8)
    mask = lax.shift_left(jnp.int32(1), bit % 8).astype(jnp.int8)
    return (octet & mask).astype(jnp.bfloat16).astype(dtype)


ORDER = (0, 4, 1, 2, 3)


def expand_kernel(r0, r1, r2, r3, r4, rhs, window, *, dtype):
    core = lax.rem(lax.axis_index("row"), 2)
    part = lax.rem(lax.axis_index("col"), 4)
    words = r0.shape[0]
    half = words // 2
    depth = words * 32
    rows = (r0, r1, r2, r3, r4)
    for k, t in enumerate(ORDER):

        def fill_rhs(w, _, k=k, t=t):
            src = lax.rem(core * half + w, words)
            at = pl.multiple_of(k * depth + w * 32, 32)
            rhs[pl.ds(at, 32), :] = zero_one(rows[t][pl.ds(src, 1), :], dtype)
            return 0

        lax.fori_loop(0, words, fill_rhs, 0, unroll=4)
    links = sum(lax.population_count(rows[t][...]) for t in range(4))
    degree = jnp.sum(links, axis=0, keepdims=True).astype(jnp.float32)
    first = jnp.where(
        part == 0,
        degree[:, :128],
        jnp.where(part == 1, degree[:, 256:384], degree[:, 512:]),
    )
    second = jnp.where(part == 0, degree[:, 128:256], degree[:, 384:512])
    window[...] = jnp.concatenate([first, second], axis=0)


def count_kernel(own, oth, r0, rhs, window, out, left, right, *, dtype, group):
    col = lax.axis_index("col")
    words, lanes = r0.shape
    depth = words * 32
    blocks = [lax.rem(col + t, 8) for t in ORDER]
    once = 2 * depth

    def fill(tile, start):
        for w in range(group):
            for k, block in enumerate(blocks):
                for side, source in enumerate((own, oth)):
                    at = k * depth + side * lanes
                    tile[w * 32 : w * 32 + 32, at : at + lanes] = scaled_bits(
                        source[block, pl.ds(start + w, 1), :], dtype
                    )

    bit = lax.broadcasted_iota(jnp.int32, (32, lanes), 0)
    spot = lax.shift_left(jnp.int32(1), bit)
    octave = lax.shift_left(jnp.int32(1), bit % 8).astype(jnp.float32)
    undo = jnp.where(bit % 8 == 7, -1.0, 1.0) / octave

    def use(tile, start, total):
        paths = jnp.dot(
            tile[:, :once], rhs[:once, :], preferred_element_type=jnp.float32
        ) + 2.0 * jnp.dot(
            tile[:, once:], rhs[once:, :], preferred_element_type=jnp.float32
        )
        for w in range(group):
            hit = (r0[pl.ds(start + w, 1), :] & spot) != 0
            picked = jnp.where(hit, paths[w * 32 : w * 32 + 32] * undo, 0.0)
            total = total + picked.reshape(4, 8, lanes).sum(axis=0)
        return total

    fill(left, 0)

    def pair(step, total):
        start = step * 2 * group
        fill(right, start + group)
        total = use(left, start, total)
        fill(left, lax.rem(start + 2 * group, words))
        return use(right, start + group, total)

    total = lax.fori_loop(
        0, words // (2 * group), pair, jnp.zeros((8, lanes), jnp.float32)
    )
    closed = jnp.sum(total, axis=0, keepdims=True)
    payload = jnp.concatenate(
        [closed[:, 128 * j : 128 * j + 128] for j in range(5)]
        + [window[...], window[:1, :]],
        axis=0,
    )
    out[...] = jnp.broadcast_to(payload[None], out.shape)


def finish_kernel(parts, relabel, clustering, transitivity):
    value = parts[...].reshape(16, 8, 8, 128)
    closed = value[:, :, :5].sum(axis=1)
    slots = [value[:, m, 5:7] + value[:, m + 4, 5:7] for m in range(3)]
    degree = jnp.concatenate([slots[0], slots[1], slots[2][:, :1]], axis=1)
    wedges = jnp.maximum(degree * (degree - 1.0), 1.0)
    ratio = (closed / wedges).reshape(80, 128)
    index = relabel[...]
    line = index // 128
    lane = index - line * 128
    hot = (lax.broadcasted_iota(jnp.int32, (128, 80), 0) == lane).astype(jnp.float32)
    picked = jnp.dot(
        ratio, hot, preferred_element_type=jnp.float32, precision=lax.Precision.HIGHEST
    )
    mine = lax.broadcasted_iota(jnp.int32, (80, 80), 0) == line
    clustering[...] = jnp.sum(jnp.where(mine, picked, 0.0), axis=0, keepdims=True)
    total = jnp.sum(closed.reshape(80, 128), axis=0, keepdims=True)
    pairs = jnp.sum(wedges.reshape(80, 128), axis=0, keepdims=True)
    transitivity[...] = jnp.sum(total, axis=1, keepdims=True) / jnp.sum(
        pairs, axis=1, keepdims=True
    )


def body(adjacency, relabel, dtype=jnp.float8_e4m3fn, group=10):
    words = adjacency.T
    cores = [[2 * chip + core for chip in range(8)] for core in range(2)]
    own = lax.all_to_all(
        spread(words, 8), "row", 0, 0, axis_index_groups=cores, tiled=True
    )
    rows = [words]
    for t in range(1, WINDOW):
        rows.append(lax.ppermute(words, "col", [((c + t) % 8, c) for c in range(8)]))
    oth = lax.ppermute(own, "row", [(r, r ^ 1) for r in range(16)])
    vmem = pl.BlockSpec(memory_space=pltpu.VMEM)
    depth = words.shape[0] * 32
    lanes = words.shape[1]

    def expand(*refs):
        expand_kernel(*refs, dtype=dtype)

    def count(*refs):
        count_kernel(*refs, dtype=dtype, group=group)

    rhs, window = pl.pallas_call(
        expand,
        out_shape=(
            jax.ShapeDtypeStruct((WINDOW * depth, lanes), dtype),
            jax.ShapeDtypeStruct((2, 128), jnp.float32),
        ),
        in_specs=[vmem] * WINDOW,
        out_specs=(vmem, vmem),
        compiler_params=pltpu.CompilerParams(vmem_limit_bytes=12 * 2**20),
        cost_estimate=pl.CostEstimate(
            flops=10**9, bytes_accessed=5 * 10**6, transcendentals=0
        ),
        name="expand",
    )(*rows)
    payload = pl.pallas_call(
        count,
        out_shape=jax.ShapeDtypeStruct((128, 8, 128), jnp.float32),
        in_specs=[vmem] * 5,
        out_specs=vmem,
        scratch_shapes=[
            pltpu.VMEM((group * 32, WINDOW * depth), dtype),
            pltpu.VMEM((group * 32, WINDOW * depth), dtype),
        ],
        compiler_params=pltpu.CompilerParams(vmem_limit_bytes=30 * 2**20),
        name="count",
    )(own, oth, words, rhs, window)
    parts = lax.all_to_all(payload, ALL, 0, 0, tiled=True)
    clustering, transitivity = pl.pallas_call(
        finish_kernel,
        out_shape=(
            jax.ShapeDtypeStruct((1, 80), jnp.float32),
            jax.ShapeDtypeStruct((1, 1), jnp.float32),
        ),
        in_specs=[vmem] * 2,
        out_specs=(vmem, vmem),
        name="finish",
    )(parts, relabel[None])
    return clustering[0], transitivity[0, 0]


def solution(mesh):
    return jax.shard_map(
        body,
        mesh=mesh,
        in_specs=(P("row", "col"), P(ALL)),
        out_specs=(P(ALL), P()),
        check_vma=False,
    )
```

time: 91.2 us -> 72.2 us (0.79)
  Pallas kernels: 29.5 us -> 12.6 us
  local copies, waits for them, and re-layouts: 4.8 us -> 1.91 us
    pallas_call x1 -> x2, Pallas kernels: 27.5 us -> 10.8 us  [the longest x1 7.95 us: body(): pl.pallas_call(count, out_shape=jax.ShapeDtypeStruct((128, 8, 128), jnp.f...]
    all_to_all x1 -> x0, local copies, waits for them, and re-layouts: 1.49 us -> none  [body(): parts = lax.all_to_all(payload, ALL, 0, 0, tiled=True)]
    unnamed x15 -> x4, local copies, waits for them, and re-layouts: 2.36 us -> 0.9 us
  transfers between devices with their start and end apart: 5 -> 5, of which waited for: 3 -> 3; matrix products, arithmetic and copies ran while one was open for 0% -> 0% of each run, Pallas kernels for 0% -> 4%
where the time goes in v2:
time: 72.2 us; the launch traced here: 71.9 us
  blocking collectives  38.4 us (53%)
  starting transfers between devices  12.7 us (18%)
  Pallas kernels  12.6 us (17%)
  waiting for transfers between devices  5.54 us (8%)
  local copies, waits for them, and re-layouts  1.91 us (3%)
    all_to_all x1, blocking collectives, body(): parts = lax.all_to_all(payload, ALL, 0, 0, tiled=True)  20.5 us
    all_to_all x1, blocking collectives, body(): lax.all_to_all(spread(words, 8), 'row', 0, 0, axis_index_groups=cores, ti...  17.9 us
    ppermute x4, starting transfers between devices, body(): lax.ppermute(words, 'col', [((c + t) % 8, c) for c in range(8)])  10.5 us
    pallas_call x1, Pallas kernels, body(): pl.pallas_call(count, out_shape=jax.ShapeDtypeStruct((128, 8, 128), jnp.f...  7.95 us
    ppermute x4, waiting for transfers between devices, body(): lax.ppermute(words, 'col', [((c + t) % 8, c) for c in range(8)])  5.54 us
    pallas_call x1, Pallas kernels, body(): pl.pallas_call(expand, out_shape=(jax.ShapeDtypeStruct((WINDOW * depth, l...  2.84 us
    ppermute x1, starting transfers between devices, body(): oth = lax.ppermute(own, 'row', [(r, r ^ 1) for r in range(16)])  2.19 us
    pallas_call x1, Pallas kernels, body(): pl.pallas_call(finish_kernel, out_shape=(jax.ShapeDtypeStruct((1, 80), jn...  1.86 us
  transfers between devices with their start and end apart: 5, of which 3 were waited for; matrix products, arithmetic and copies ran while one was open for 0% of the time, Pallas kernels for 4%

profile of v2, /device:TPU:1, one launch (start us, length us, event | category | flops | bytes accessed | tf_op | source)
XLA Modules:
  0.0 71.9 jit_solution(15122627097718250409)
XLA Ops:
  0.6 0.0 copy-start.1
  0.6 1.0 %broadcast_in_dim.4 = s32[8,40,640]{2,1,0:T(8,128)S(1)} broadcast(s32[40,640]{1,0:T(8,128)} %bitcast.4), dimensions={1,2} | broadcast | bytes 921600 | tf_op jit(solution)/shard_map/broadcast_in_dim | solution.py:13
  1.7 17.9 %all_to_all.10.refs_0_ = s32[8,40,640]{2,1,0:T(8,128)S(1)} all-to-all(s32[8,40,640]{2,1,0:T(8,128)S(1)} %broadcast_in_dim.4), channel_id=1, replica_groups={{0,16,32,48,64,80,96,112},{8,24,40,56,72,88,104,120},{1,17,33,49,65,81,..., dimensions={0} | all-to-all | bytes 1638400 | tf_op jit(solution)/shard_map/all_to_all | solution.py:144
  19.6 2.2 %collective-permute-start = (s32[8,40,640]{2,1,0:T(8,128)S(1)}, s32[8,40,640]{2,1,0:T(8,128)S(1)}, u32[]{:S(2)}, u32[]{:S(2)}) collective-permute-start(s32[8,40,640]{2,1,0:T(8,128)S(1)} %all_to_all.10.refs_0_), channel_id=1, source_target_pairs={{0,8},{8,0},{16,24},{24,16},{32,40},{40,32},{48,56},{56,48},{64,72... | collective-permute-start | bytes 2457608 | tf_op jit(solution)/shard_map/ppermute | solution.py:150
  21.8 2.5 %collective-permute-start.4 = (s32[40,640]{1,0:T(8,128)}, s32[40,640]{1,0:T(8,128)S(1)}, u32[]{:S(2)}, u32[]{:S(2)}) collective-permute-start(s32[40,640]{1,0:T(8,128)} %bitcast.5), channel_id=1, source_target_pairs={{4,0},{5,1},{6,2},{7,3},{0,4},{1,5},{2,6},{3,7},{12,8},{13,9},{14,... | collective-permute-start | bytes 307208 | tf_op jit(solution)/shard_map/ppermute | solution.py:149
  24.2 1.9 %collective-permute-start.3 = (s32[40,640]{1,0:T(8,128)}, s32[40,640]{1,0:T(8,128)S(1)}, u32[]{:S(2)}, u32[]{:S(2)}) collective-permute-start(s32[40,640]{1,0:T(8,128)} %bitcast.6), channel_id=1, source_target_pairs={{3,0},{4,1},{5,2},{6,3},{7,4},{0,5},{1,6},{2,7},{11,8},{12,9},{13,... | collective-permute-start | bytes 307208 | tf_op jit(solution)/shard_map/ppermute | solution.py:149
  26.1 5.5 %collective-permute-start.2 = (s32[40,640]{1,0:T(8,128)}, s32[40,640]{1,0:T(8,128)S(1)}, u32[]{:S(2)}, u32[]{:S(2)}) collective-permute-start(s32[40,640]{1,0:T(8,128)} %bitcast.7), channel_id=1, source_target_pairs={{2,0},{3,1},{4,2},{5,3},{6,4},{7,5},{0,6},{1,7},{10,8},{11,9},{12,... | collective-permute-start | bytes 307208 | tf_op jit(solution)/shard_map/ppermute | solution.py:149
  31.6 0.7 %collective-permute-start.1 = (s32[40,640]{1,0:T(8,128)}, s32[40,640]{1,0:T(8,128)S(1)}, u32[]{:S(2)}, u32[]{:S(2)}) collective-permute-start(s32[40,640]{1,0:T(8,128)} %bitcast.8), channel_id=1, source_target_pairs={{1,0},{2,1},{3,2},{4,3},{5,4},{6,5},{7,6},{0,7},{9,8},{10,9},{11,1... | collective-permute-start | bytes 307208 | tf_op jit(solution)/shard_map/ppermute | solution.py:149
  32.3 0.0 collective-permute-done.4.refs_4_
  32.3 1.1 %collective-permute-done.3.refs_3_ = s32[40,640]{1,0:T(8,128)S(1)} collective-permute-done((s32[40,640]{1,0:T(8,128)}, s32[40,640]{1,0:T(8,128)S(1)}, u32[]{:S(2)}, u32[]{:S(2)}) %collective-permute-start.3) | collective-permute-done | bytes 102432 | tf_op jit(solution)/shard_map/ppermute | solution.py:149
  33.4 0.2 collective-permute-done.2.refs_2_
  33.6 4.3 %collective-permute-done.1.refs_1_ = s32[40,640]{1,0:T(8,128)S(1)} collective-permute-done((s32[40,640]{1,0:T(8,128)}, s32[40,640]{1,0:T(8,128)S(1)}, u32[]{:S(2)}, u32[]{:S(2)}) %collective-permute-start.1) | collective-permute-done | bytes 102432 | tf_op jit(solution)/shard_map/ppermute | solution.py:149
  37.9 0.0 copy-start
  37.9 0.9 %copy-done = s32[640,40]{0,1:T(8,128)S(1)} copy-done((s32[640,40]{0,1:T(8,128)S(1)}, s32[640,40]{0,1:T(8,128)}, u32[]{:S(2)}) %copy-start) | copy-done | bytes 102424
  38.8 2.8 %expand.1 = (f8e4m3fn[6400,640]{1,0:T(32,128)(4,1)S(1)}, f32[2,128]{1,0:T(2,128)S(1)}) custom-call(s32[40,640]{1,0:T(8,128)S(1)} %bitcast.9, s32[40,640]{1,0:T(8,128)S(1)} %collective-permute-done.1.refs_1_, s32[40,640]{1,0:T(8,128)S(1)} %collective-permute-done.2.refs_2_, s32[40,640]{1,0:T(8,128)S(1)} %collective-permute-done.3.refs_3_, ...), custom_call_target="tpu_custom_call" | custom-call | flops 1000000000 | bytes 5000000 | tf_op jit(solution)/shard_map/expand/pallas_call | solution.py:161
  41.6 0.0 collective-permute-done.refs_1_
  41.6 0.0 copy-done.1
  41.6 8.0 %count.1 = f32[128,8,128]{2,1,0:T(8,128)S(1)} custom-call(s32[8,40,640]{2,1,0:T(8,128)S(1)} %all_to_all.10.refs_0_, s32[8,40,640]{2,1,0:T(8,128)S(1)} %collective-permute-done.refs_1_, s32[40,640]{1,0:T(8,128)S(1)} %bitcast.10, f8e4m3fn[6400,640]{1,0:T(32,128)(4,1)S(1)} %get-tuple-element.6.refs_3_, f32[2,128]{1,0:T(2,128)S(1)} %get-tuple-element.7.refs_4_), custom_call_target="tpu_custom_call" | custom-call | tf_op jit(solution)/shard_map/count/pallas_call | solution.py:175
  49.6 20.5 %all_to_all.11.parts = f32[128,8,128]{2,1,0:T(8,128)} all-to-all(f32[128,8,128]{2,1,0:T(8,128)S(1)} %count.1), channel_id=1, replica_groups=mesh['row'=16,'col'=8] {'row','col'}, dimensions={0} | all-to-all | bytes 1048576 | tf_op jit(solution)/shard_map/all_to_all | solution.py:187
  70.1 1.9 %finish.1 = (f32[1,80]{1,0:T(1,128)}, f32[1,1]{1,0:T(1,128)}) custom-call(f32[128,8,128]{2,1,0:T(8,128)} %all_to_all.11.parts, s32[1,80]{1,0:T(1,128)} %bitcast.11), custom_call_target="tpu_custom_call" | custom-call | tf_op jit(solution)/shard_map/finish/pallas_call | solution.py:188
Async XLA Ops:
  0.6 41.0 %copy-start.1 = (s32[640,40]{0,1:T(8,128)S(1)}, s32[640,40]{0,1:T(8,128)}, u32[]{:S(2)}) copy-start(s32[640,40]{0,1:T(8,128)} %param.2) | copy-start | bytes 307204
  19.6 22.0 %collective-permute-start = (s32[8,40,640]{2,1,0:T(8,128)S(1)}, s32[8,40,640]{2,1,0:T(8,128)S(1)}, u32[]{:S(2)}, u32[]{:S(2)}) collective-permute-start(s32[8,40,640]{2,1,0:T(8,128)S(1)} %all_to_all.10.refs_0_), channel_id=1, source_target_pairs={{0,8},{8,0},{16,24},{24,16},{32,40},{40,32},{48,56},{56,48},{64,72... | collective-permute-start | bytes 2457608 | tf_op jit(solution)/shard_map/ppermute | solution.py:150
  21.8 10.5 %collective-permute-start.4 = (s32[40,640]{1,0:T(8,128)}, s32[40,640]{1,0:T(8,128)S(1)}, u32[]{:S(2)}, u32[]{:S(2)}) collective-permute-start(s32[40,640]{1,0:T(8,128)} %bitcast.5), channel_id=1, source_target_pairs={{4,0},{5,1},{6,2},{7,3},{0,4},{1,5},{2,6},{3,7},{12,8},{13,9},{14,... | collective-permute-start | bytes 307208 | tf_op jit(solution)/shard_map/ppermute | solution.py:149
  24.2 9.2 %collective-permute-start.3 = (s32[40,640]{1,0:T(8,128)}, s32[40,640]{1,0:T(8,128)S(1)}, u32[]{:S(2)}, u32[]{:S(2)}) collective-permute-start(s32[40,640]{1,0:T(8,128)} %bitcast.6), channel_id=1, source_target_pairs={{3,0},{4,1},{5,2},{6,3},{7,4},{0,5},{1,6},{2,7},{11,8},{12,9},{13,... | collective-permute-start | bytes 307208 | tf_op jit(solution)/shard_map/ppermute | solution.py:149
  26.1 7.5 %collective-permute-start.2 = (s32[40,640]{1,0:T(8,128)}, s32[40,640]{1,0:T(8,128)S(1)}, u32[]{:S(2)}, u32[]{:S(2)}) collective-permute-start(s32[40,640]{1,0:T(8,128)} %bitcast.7), channel_id=1, source_target_pairs={{2,0},{3,1},{4,2},{5,3},{6,4},{7,5},{0,6},{1,7},{10,8},{11,9},{12,... | collective-permute-start | bytes 307208 | tf_op jit(solution)/shard_map/ppermute | solution.py:149
  31.6 6.3 %collective-permute-start.1 = (s32[40,640]{1,0:T(8,128)}, s32[40,640]{1,0:T(8,128)S(1)}, u32[]{:S(2)}, u32[]{:S(2)}) collective-permute-start(s32[40,640]{1,0:T(8,128)} %bitcast.8), channel_id=1, source_target_pairs={{1,0},{2,1},{3,2},{4,3},{5,4},{6,5},{7,6},{0,7},{9,8},{10,9},{11,1... | collective-permute-start | bytes 307208 | tf_op jit(solution)/shard_map/ppermute | solution.py:149
  37.9 0.9 %copy-start = (s32[640,40]{0,1:T(8,128)S(1)}, s32[640,40]{0,1:T(8,128)}, u32[]{:S(2)}) copy-start(s32[640,40]{0,1:T(8,128)} %param.2) | copy-start | bytes 307204

commit v3 on v2

--- a/solution.py
+++ b/solution.py
@@ -31,42 +31,35 @@
     return (octet & mask).astype(jnp.bfloat16).astype(dtype)
 
 
-ORDER = (0, 4, 1, 2, 3)
-
-
-def expand_kernel(r0, r1, r2, r3, r4, rhs, window, *, dtype):
+ORDER = (0, 1, 4, 2, 3)
+EARLY = ORDER[:2]
+LATE = ORDER[2:]
+
+
+def expand_kernel(*refs, dtype):
     core = lax.rem(lax.axis_index("row"), 2)
-    part = lax.rem(lax.axis_index("col"), 4)
-    words = r0.shape[0]
+    rows, rhs, tally = refs[:-2], refs[-2], refs[-1]
+    words = rows[0].shape[0]
     half = words // 2
     depth = words * 32
-    rows = (r0, r1, r2, r3, r4)
-    for k, t in enumerate(ORDER):
-
-        def fill_rhs(w, _, k=k, t=t):
+    for k, row in enumerate(rows):
+
+        def fill_rhs(w, _, k=k, row=row):
             src = lax.rem(core * half + w, words)
             at = pl.multiple_of(k * depth + w * 32, 32)
-            rhs[pl.ds(at, 32), :] = zero_one(rows[t][pl.ds(src, 1), :], dtype)
+            rhs[pl.ds(at, 32), :] = zero_one(row[pl.ds(src, 1), :], dtype)
             return 0
 
         lax.fori_loop(0, words, fill_rhs, 0, unroll=4)
-    links = sum(lax.population_count(rows[t][...]) for t in range(4))
-    degree = jnp.sum(links, axis=0, keepdims=True).astype(jnp.float32)
-    first = jnp.where(
-        part == 0,
-        degree[:, :128],
-        jnp.where(part == 1, degree[:, 256:384], degree[:, 512:]),
-    )
-    second = jnp.where(part == 0, degree[:, 128:256], degree[:, 384:512])
-    window[...] = jnp.concatenate([first, second], axis=0)
-
-
-def count_kernel(own, oth, r0, rhs, window, out, left, right, *, dtype, group):
+    links = sum(lax.population_count(row[...]) for row in rows[-2:])
+    tally[...] = jnp.sum(links, axis=0, keepdims=True).astype(jnp.float32)
+
+
+def count_kernel(own, oth, r0, early, late, near, far, out, left, right, *, dtype, group):
     col = lax.axis_index("col")
     words, lanes = r0.shape
     depth = words * 32
     blocks = [lax.rem(col + t, 8) for t in ORDER]
-    once = 2 * depth
 
     def fill(tile, start):
         for w in range(group):
@@ -83,11 +76,15 @@
     undo = jnp.where(bit % 8 == 7, -1.0, 1.0) / octave
 
     def use(tile, start, total):
-        paths = jnp.dot(
-            tile[:, :once], rhs[:once, :], preferred_element_type=jnp.float32
-        ) + 2.0 * jnp.dot(
-            tile[:, once:], rhs[once:, :], preferred_element_type=jnp.float32
-        )
+        def times(first, rhs):
+            count = rhs.shape[0]
+            return jnp.dot(
+                tile[:, first : first + count], rhs, preferred_element_type=jnp.float32
+            )
+
+        doubled = times(depth, early[depth:, :]) + times(3 * depth, late[depth:, :])
+        paths = times(0, early[:depth, :]) + times(2 * depth, late[:depth, :])
+        paths = paths + 2.0 * doubled
         for w in range(group):
             hit = (r0[pl.ds(start + w, 1), :] & spot) != 0
             picked = jnp.where(hit, paths[w * 32 : w * 32 + 32] * undo, 0.0)
@@ -107,9 +104,16 @@
         0, words // (2 * group), pair, jnp.zeros((8, lanes), jnp.float32)
     )
     closed = jnp.sum(total, axis=0, keepdims=True)
+    degree = near[...] + far[...]
+    part = lax.rem(col, 4)
+    first = jnp.where(
+        part == 0,
+        degree[:, :128],
+        jnp.where(part == 1, degree[:, 256:384], degree[:, 512:]),
+    )
+    second = jnp.where(part == 0, degree[:, 128:256], degree[:, 384:512])
     payload = jnp.concatenate(
-        [closed[:, 128 * j : 128 * j + 128] for j in range(5)]
-        + [window[...], window[:1, :]],
+        [closed[:, 128 * j : 128 * j + 128] for j in range(5)] + [first, second, first],
         axis=0,
     )
     out[...] = jnp.broadcast_to(payload[None], out.shape)
@@ -152,30 +156,33 @@
     depth = words.shape[0] * 32
     lanes = words.shape[1]
 
-    def expand(*refs):
-        expand_kernel(*refs, dtype=dtype)
-
     def count(*refs):
         count_kernel(*refs, dtype=dtype, group=group)
 
-    rhs, window = pl.pallas_call(
-        expand,
-        out_shape=(
-            jax.ShapeDtypeStruct((WINDOW * depth, lanes), dtype),
-            jax.ShapeDtypeStruct((2, 128), jnp.float32),
-        ),
-        in_specs=[vmem] * WINDOW,
-        out_specs=(vmem, vmem),
-        compiler_params=pltpu.CompilerParams(vmem_limit_bytes=12 * 2**20),
-        cost_estimate=pl.CostEstimate(
-            flops=10**9, bytes_accessed=5 * 10**6, transcendentals=0
-        ),
-        name="expand",
-    )(*rows)
+    def expand(picks):
+        def kernel(*refs):
+            expand_kernel(*refs, dtype=dtype)
+
+        return pl.pallas_call(
+            kernel,
+            out_shape=(
+                jax.ShapeDtypeStruct((len(picks) * depth, lanes), dtype),
+                jax.ShapeDtypeStruct((1, lanes), jnp.float32),
+            ),
+            in_specs=[vmem] * len(picks),
+            out_specs=(vmem, vmem),
+            compiler_params=pltpu.CompilerParams(vmem_limit_bytes=12 * 2**20),
+            cost_estimate=pl.CostEstimate(
+                flops=4 * 10**8, bytes_accessed=3 * 10**6, transcendentals=0
+            ),
+        )(*[rows[t] for t in picks])
+
+    early, near = expand(EARLY)
+    late, far = expand(LATE)
     payload = pl.pallas_call(
         count,
         out_shape=jax.ShapeDtypeStruct((128, 8, 128), jnp.float32),
-        in_specs=[vmem] * 5,
+        in_specs=[vmem] * 7,
         out_specs=vmem,
         scratch_shapes=[
             pltpu.VMEM((group * 32, WINDOW * depth), dtype),
@@ -183,7 +190,7 @@
         ],
         compiler_params=pltpu.CompilerParams(vmem_limit_bytes=30 * 2**20),
         name="count",
-    )(own, oth, words, rhs, window)
+    )(own, oth, words, early, late, near, far)
     parts = lax.all_to_all(payload, ALL, 0, 0, tiled=True)
     clustering, transitivity = pl.pallas_call(
         finish_kernel,

time: 72.2 us -> 69.3 us (0.960)
  blocking collectives: 38.4 us -> 37.4 us
  local copies, waits for them, and re-layouts: 1.91 us -> 1.02 us
    all_to_all x1, blocking collectives: 20.5 us -> 19.4 us  [body(): parts = lax.all_to_all(payload, ALL, 0, 0, tiled=True)]
    unnamed x4 -> x2, local copies, waits for them, and re-layouts: 0.9 us -> 0.01 us
    pallas_call x1 -> x2, Pallas kernels: 2.84 us -> 2.82 us  [expand(): pl.pallas_call(kernel, out_shape=(jax.ShapeDtypeStruct((len(picks) * dept...]
  transfers between devices with their start and end apart: 5 -> 5, of which waited for: 3 -> 2; matrix products, arithmetic and copies ran while one was open for 0% -> 0% of each run, Pallas kernels for 4% -> 4%
where the time goes in v3:
time: 69.3 us; the launch traced here: 69.1 us
  blocking collectives  37.4 us (54%)
  Pallas kernels  13 us (19%)
  starting transfers between devices  12.1 us (17%)
  waiting for transfers between devices  4.95 us (7%)
  local copies, waits for them, and re-layouts  1.02 us (1%)
    all_to_all x1, blocking collectives, body(): parts = lax.all_to_all(payload, ALL, 0, 0, tiled=True)  19.4 us
    all_to_all x1, blocking collectives, body(): lax.all_to_all(spread(words, 8), 'row', 0, 0, axis_index_groups=cores, ti...  17.9 us
    ppermute x4, starting transfers between devices, body(): lax.ppermute(words, 'col', [((c + t) % 8, c) for c in range(8)])  9.92 us
    pallas_call x1, Pallas kernels, body(): pl.pallas_call(count, out_shape=jax.ShapeDtypeStruct((128, 8, 128), jnp.f...  8.31 us
    ppermute x4, waiting for transfers between devices, body(): lax.ppermute(words, 'col', [((c + t) % 8, c) for c in range(8)])  4.95 us
    pallas_call x2, Pallas kernels, expand(): pl.pallas_call(kernel, out_shape=(jax.ShapeDtypeStruct((len(picks) * dept...  2.82 us
    ppermute x1, starting transfers between devices, body(): oth = lax.ppermute(own, 'row', [(r, r ^ 1) for r in range(16)])  2.19 us
    pallas_call x1, Pallas kernels, body(): pl.pallas_call(finish_kernel, out_shape=(jax.ShapeDtypeStruct((1, 80), jn...  1.86 us
  transfers between devices with their start and end apart: 5, of which 2 were waited for; matrix products, arithmetic and copies ran while one was open for 0% of the time, Pallas kernels for 4%

profile of v3, /device:TPU:1, one launch (start us, length us, event | category | flops | bytes accessed | tf_op | source)
XLA Modules:
  0.0 69.1 jit_solution(2036866095027962772)
XLA Ops:
  0.6 0.0 copy-start
  0.6 1.0 %broadcast_in_dim.4 = s32[8,40,640]{2,1,0:T(8,128)S(1)} broadcast(s32[40,640]{1,0:T(8,128)} %bitcast.4), dimensions={1,2} | broadcast | bytes 921600 | tf_op jit(solution)/shard_map/broadcast_in_dim | solution.py:13
  1.7 17.9 %all_to_all.10.refs_0_ = s32[8,40,640]{2,1,0:T(8,128)S(1)} all-to-all(s32[8,40,640]{2,1,0:T(8,128)S(1)} %broadcast_in_dim.4), channel_id=1, replica_groups={{0,16,32,48,64,80,96,112},{8,24,40,56,72,88,104,120},{1,17,33,49,65,81,..., dimensions={0} | all-to-all | bytes 1638400 | tf_op jit(solution)/shard_map/all_to_all | solution.py:148
  19.6 2.2 %collective-permute-start = (s32[8,40,640]{2,1,0:T(8,128)S(1)}, s32[8,40,640]{2,1,0:T(8,128)S(1)}, u32[]{:S(2)}, u32[]{:S(2)}) collective-permute-start(s32[8,40,640]{2,1,0:T(8,128)S(1)} %all_to_all.10.refs_0_), channel_id=1, source_target_pairs={{0,8},{8,0},{16,24},{24,16},{32,40},{40,32},{48,56},{56,48},{64,72... | collective-permute-start | bytes 2457608 | tf_op jit(solution)/shard_map/ppermute | solution.py:154
  21.8 0.0 copy-done
  21.8 5.9 %collective-permute-start.1 = (s32[40,640]{1,0:T(8,128)S(1)}, s32[40,640]{1,0:T(8,128)S(1)}, u32[]{:S(2)}, u32[]{:S(2)}) collective-permute-start(s32[40,640]{1,0:T(8,128)S(1)} %bitcast.5), channel_id=1, source_target_pairs={{1,0},{2,1},{3,2},{4,3},{5,4},{6,5},{7,6},{0,7},{9,8},{10,9},{11,1... | collective-permute-start | bytes 307208 | tf_op jit(solution)/shard_map/ppermute | solution.py:153
  27.7 0.0 collective-permute-start.4
  27.7 1.5 %collective-permute-start.3 = (s32[40,640]{1,0:T(8,128)S(1)}, s32[40,640]{1,0:T(8,128)S(1)}, u32[]{:S(2)}, u32[]{:S(2)}) collective-permute-start(s32[40,640]{1,0:T(8,128)S(1)} %bitcast.7), channel_id=1, source_target_pairs={{2,0},{3,1},{4,2},{5,3},{6,4},{7,5},{0,6},{1,7},{10,8},{11,9},{12,... | collective-permute-start | bytes 307208 | tf_op jit(solution)/shard_map/ppermute | solution.py:153
  29.3 2.5 %collective-permute-start.2 = (s32[40,640]{1,0:T(8,128)S(1)}, s32[40,640]{1,0:T(8,128)S(1)}, u32[]{:S(2)}, u32[]{:S(2)}) collective-permute-start(s32[40,640]{1,0:T(8,128)S(1)} %bitcast.8), channel_id=1, source_target_pairs={{4,0},{5,1},{6,2},{7,3},{0,4},{1,5},{2,6},{3,7},{12,8},{13,9},{14,... | collective-permute-start | bytes 307208 | tf_op jit(solution)/shard_map/ppermute | solution.py:153
  31.7 0.0 collective-permute-done.1.refs_1_
  31.7 1.1 %shard_map.41 = (f8e4m3fn[2560,640]{1,0:T(32,128)(4,1)S(1)}, f32[1,640]{1,0:T(1,128)S(1)}) custom-call(s32[40,640]{1,0:T(8,128)S(1)} %bitcast.9, s32[40,640]{1,0:T(8,128)S(1)} %collective-permute-done.1.refs_1_), custom_call_target="tpu_custom_call" | custom-call | flops 400000000 | bytes 3000000 | tf_op jit(solution)/shard_map/pallas_call | solution.py:166
  32.8 2.5 %collective-permute-done.4.refs_2_ = s32[40,640]{1,0:T(8,128)S(1)} collective-permute-done((s32[40,640]{1,0:T(8,128)S(1)}, s32[40,640]{1,0:T(8,128)S(1)}, u32[]{:S(2)}, u32[]{:S(2)}) %collective-permute-start.4) | collective-permute-done | bytes 102432 | tf_op jit(solution)/shard_map/ppermute | solution.py:153
  35.3 0.0 collective-permute-done.3.refs_1_
  35.3 2.5 %collective-permute-done.2.refs_0_ = s32[40,640]{1,0:T(8,128)S(1)} collective-permute-done((s32[40,640]{1,0:T(8,128)S(1)}, s32[40,640]{1,0:T(8,128)S(1)}, u32[]{:S(2)}, u32[]{:S(2)}) %collective-permute-start.2) | collective-permute-done | bytes 102432 | tf_op jit(solution)/shard_map/ppermute | solution.py:153
  37.8 1.7 %shard_map.42 = (f8e4m3fn[3840,640]{1,0:T(32,128)(4,1)S(1)}, f32[1,640]{1,0:T(1,128)S(1)}) custom-call(s32[40,640]{1,0:T(8,128)S(1)} %collective-permute-done.2.refs_0_, s32[40,640]{1,0:T(8,128)S(1)} %collective-permute-done.3.refs_1_, s32[40,640]{1,0:T(8,128)S(1)} %collective-permute-done.4.refs_2_), custom_call_target="tpu_custom_call" | custom-call | flops 400000000 | bytes 3000000 | tf_op jit(solution)/shard_map/pallas_call | solution.py:166
  39.5 0.0 collective-permute-done.refs_1_
  39.5 8.3 %count.1 = f32[128,8,128]{2,1,0:T(8,128)S(1)} custom-call(s32[8,40,640]{2,1,0:T(8,128)S(1)} %all_to_all.10.refs_0_, s32[8,40,640]{2,1,0:T(8,128)S(1)} %collective-permute-done.refs_1_, s32[40,640]{1,0:T(8,128)S(1)} %bitcast.10, f8e4m3fn[2560,640]{1,0:T(32,128)(4,1)S(1)} %get-tuple-element.8.refs_3_, f8e4m3fn[3840,640]{1,0:T(32,128)(4,1)S(1)} %get-tuple-element.9.refs_4_, ...), custom_call_target="tpu_custom_call" | custom-call | tf_op jit(solution)/shard_map/count/pallas_call | solution.py:182
  47.8 19.4 %all_to_all.11.parts = f32[128,8,128]{2,1,0:T(8,128)} all-to-all(f32[128,8,128]{2,1,0:T(8,128)S(1)} %count.1), channel_id=1, replica_groups=mesh['row'=16,'col'=8] {'row','col'}, dimensions={0} | all-to-all | bytes 1048576 | tf_op jit(solution)/shard_map/all_to_all | solution.py:194
  67.2 1.9 %finish.1 = (f32[1,80]{1,0:T(1,128)}, f32[1,1]{1,0:T(1,128)}) custom-call(f32[128,8,128]{2,1,0:T(8,128)} %all_to_all.11.parts, s32[1,80]{1,0:T(1,128)} %bitcast.11), custom_call_target="tpu_custom_call" | custom-call | tf_op jit(solution)/shard_map/finish/pallas_call | solution.py:195
Async XLA Ops:
  0.6 21.2 %copy-start = (s32[640,40]{0,1:T(8,128)S(1)}, s32[640,40]{0,1:T(8,128)}, u32[]{:S(2)}) copy-start(s32[640,40]{0,1:T(8,128)} %param.2) | copy-start | bytes 307204
  19.6 19.9 %collective-permute-start = (s32[8,40,640]{2,1,0:T(8,128)S(1)}, s32[8,40,640]{2,1,0:T(8,128)S(1)}, u32[]{:S(2)}, u32[]{:S(2)}) collective-permute-start(s32[8,40,640]{2,1,0:T(8,128)S(1)} %all_to_all.10.refs_0_), channel_id=1, source_target_pairs={{0,8},{8,0},{16,24},{24,16},{32,40},{40,32},{48,56},{56,48},{64,72... | collective-permute-start | bytes 2457608 | tf_op jit(solution)/shard_map/ppermute | solution.py:154
  21.8 9.9 %collective-permute-start.1 = (s32[40,640]{1,0:T(8,128)S(1)}, s32[40,640]{1,0:T(8,128)S(1)}, u32[]{:S(2)}, u32[]{:S(2)}) collective-permute-start(s32[40,640]{1,0:T(8,128)S(1)} %bitcast.5), channel_id=1, source_target_pairs={{1,0},{2,1},{3,2},{4,3},{5,4},{6,5},{7,6},{0,7},{9,8},{10,9},{11,1... | collective-permute-start | bytes 307208 | tf_op jit(solution)/shard_map/ppermute | solution.py:153
  27.7 7.6 %collective-permute-start.4 = (s32[40,640]{1,0:T(8,128)S(1)}, s32[40,640]{1,0:T(8,128)S(1)}, u32[]{:S(2)}, u32[]{:S(2)}) collective-permute-start(s32[40,640]{1,0:T(8,128)S(1)} %bitcast.6), channel_id=1, source_target_pairs={{3,0},{4,1},{5,2},{6,3},{7,4},{0,5},{1,6},{2,7},{11,8},{12,9},{13,... | collective-permute-start | bytes 307208 | tf_op jit(solution)/shard_map/ppermute | solution.py:153
  27.7 7.6 %collective-permute-start.3 = (s32[40,640]{1,0:T(8,128)S(1)}, s32[40,640]{1,0:T(8,128)S(1)}, u32[]{:S(2)}, u32[]{:S(2)}) collective-permute-start(s32[40,640]{1,0:T(8,128)S(1)} %bitcast.7), channel_id=1, source_target_pairs={{2,0},{3,1},{4,2},{5,3},{6,4},{7,5},{0,6},{1,7},{10,8},{11,9},{12,... | collective-permute-start | bytes 307208 | tf_op jit(solution)/shard_map/ppermute | solution.py:153
  29.3 8.5 %collective-permute-start.2 = (s32[40,640]{1,0:T(8,128)S(1)}, s32[40,640]{1,0:T(8,128)S(1)}, u32[]{:S(2)}, u32[]{:S(2)}) collective-permute-start(s32[40,640]{1,0:T(8,128)S(1)} %bitcast.8), channel_id=1, source_target_pairs={{4,0},{5,1},{6,2},{7,3},{0,4},{1,5},{2,6},{3,7},{12,8},{13,9},{14,... | collective-permute-start | bytes 307208 | tf_op jit(solution)/shard_map/ppermute | solution.py:153

commit v4 on v3

--- a/solution.py
+++ b/solution.py
@@ -55,39 +55,48 @@
     tally[...] = jnp.sum(links, axis=0, keepdims=True).astype(jnp.float32)
 
 
-def count_kernel(own, oth, r0, early, late, near, far, out, left, right, *, dtype, group):
+def count_kernel(*refs, picks, weights, group, finish):
+    own, oth = refs[:2]
+    rhs = refs[2]
+    out, left, right = refs[-3:]
     col = lax.axis_index("col")
-    words, lanes = r0.shape
+    blocks, words, lanes = own.shape
     depth = words * 32
-    blocks = [lax.rem(col + t, 8) for t in ORDER]
+    places = [lax.rem(col + t, blocks) for t in picks]
+    if finish:
+        mask, paths_in, near, far = refs[3:7]
+        bit = lax.broadcasted_iota(jnp.int32, (32, lanes), 0)
+        spot = lax.shift_left(jnp.int32(1), bit)
+        octave = lax.shift_left(jnp.int32(1), bit % 8).astype(jnp.float32)
+        undo = jnp.where(bit % 8 == 7, -1.0, 1.0) / octave
 
     def fill(tile, start):
         for w in range(group):
-            for k, block in enumerate(blocks):
+            for k, place in enumerate(places):
                 for side, source in enumerate((own, oth)):
                     at = k * depth + side * lanes
                     tile[w * 32 : w * 32 + 32, at : at + lanes] = scaled_bits(
-                        source[block, pl.ds(start + w, 1), :], dtype
+                        source[place, pl.ds(start + w, 1), :], tile.dtype
                     )
 
-    bit = lax.broadcasted_iota(jnp.int32, (32, lanes), 0)
-    spot = lax.shift_left(jnp.int32(1), bit)
-    octave = lax.shift_left(jnp.int32(1), bit % 8).astype(jnp.float32)
-    undo = jnp.where(bit % 8 == 7, -1.0, 1.0) / octave
-
     def use(tile, start, total):
-        def times(first, rhs):
-            count = rhs.shape[0]
-            return jnp.dot(
-                tile[:, first : first + count], rhs, preferred_element_type=jnp.float32
+        paths = 0.0
+        first = 0
+        for weight in dict.fromkeys(weights):
+            last = first + weights.count(weight) * depth
+            paths = paths + weight * jnp.dot(
+                tile[:, first:last], rhs[first:last, :], preferred_element_type=jnp.float32
             )
-
-        doubled = times(depth, early[depth:, :]) + times(3 * depth, late[depth:, :])
-        paths = times(0, early[:depth, :]) + times(2 * depth, late[:depth, :])
-        paths = paths + 2.0 * doubled
+            first = last
+        at = pl.multiple_of(start * 32, 32)
+        if not finish:
+            out[pl.ds(at, group * 32), :] = paths
+            return total
         for w in range(group):
-            hit = (r0[pl.ds(start + w, 1), :] & spot) != 0
-            picked = jnp.where(hit, paths[w * 32 : w * 32 + 32] * undo, 0.0)
+            hit = (mask[pl.ds(start + w, 1), :] & spot) != 0
+            known = paths_in[pl.ds(pl.multiple_of(at + w * 32, 32), 32), :]
+            value = (paths[w * 32 : w * 32 + 32] + known) * undo
+            picked = jnp.where(hit, value, 0.0)
             total = total + picked.reshape(4, 8, lanes).sum(axis=0)
         return total
 
@@ -103,6 +112,8 @@
     total = lax.fori_loop(
         0, words // (2 * group), pair, jnp.zeros((8, lanes), jnp.float32)
     )
+    if not finish:
+        return
     closed = jnp.sum(total, axis=0, keepdims=True)
     degree = near[...] + far[...]
     part = lax.rem(col, 4)
@@ -156,9 +167,6 @@
     depth = words.shape[0] * 32
     lanes = words.shape[1]
 
-    def count(*refs):
-        count_kernel(*refs, dtype=dtype, group=group)
-
     def expand(picks):
         def kernel(*refs):
             expand_kernel(*refs, dtype=dtype)
@@ -179,18 +187,34 @@
 
     early, near = expand(EARLY)
     late, far = expand(LATE)
-    payload = pl.pallas_call(
-        count,
-        out_shape=jax.ShapeDtypeStruct((128, 8, 128), jnp.float32),
-        in_specs=[vmem] * 7,
-        out_specs=vmem,
-        scratch_shapes=[
-            pltpu.VMEM((group * 32, WINDOW * depth), dtype),
-            pltpu.VMEM((group * 32, WINDOW * depth), dtype),
-        ],
-        compiler_params=pltpu.CompilerParams(vmem_limit_bytes=30 * 2**20),
-        name="count",
-    )(own, oth, words, early, late, near, far)
+
+    def count(picks, weights, operands, out_shape, finish):
+        def kernel(*refs):
+            count_kernel(*refs, picks=picks, weights=weights, group=group, finish=finish)
+
+        tile = pltpu.VMEM((group * 32, len(picks) * depth), dtype)
+        return pl.pallas_call(
+            kernel,
+            out_shape=jax.ShapeDtypeStruct(out_shape, jnp.float32),
+            in_specs=[vmem] * len(operands),
+            out_specs=vmem,
+            scratch_shapes=[tile, tile],
+            compiler_params=pltpu.CompilerParams(vmem_limit_bytes=24 * 2**20),
+            cost_estimate=pl.CostEstimate(
+                flops=2 * len(picks) * depth * depth * lanes,
+                bytes_accessed=6 * 10**6,
+                transcendentals=0,
+            ),
+        )(*operands)
+
+    paths = count(EARLY, (1.0, 2.0), (own, oth, early), (depth, lanes), False)
+    payload = count(
+        LATE,
+        (1.0, 2.0, 2.0),
+        (own, oth, late, words, paths, near, far),
+        (128, 8, 128),
+        True,
+    )
     parts = lax.all_to_all(payload, ALL, 0, 0, tiled=True)
     clustering, transitivity = pl.pallas_call(
         finish_kernel,
@@ -200,6 +224,7 @@
         ),
         in_specs=[vmem] * 2,
         out_specs=(vmem, vmem),
+        compiler_params=pltpu.CompilerParams(vmem_limit_bytes=4 * 2**20),
         name="finish",
     )(parts, relabel[None])
     return clustering[0], transitivity[0, 0]

time: 69.3 us -> 68.2 us (0.984)
  Pallas kernels: 13 us -> 12 us
    pallas_call x1, Pallas kernels: 1.86 us -> 0.81 us  [body(): pl.pallas_call(finish_kernel, out_shape=(jax.ShapeDtypeStruct((1, 80), jn...]
    pallas_call x1 -> x2, Pallas kernels: 8.31 us -> 8.35 us  [count(): pl.pallas_call(kernel, out_shape=jax.ShapeDtypeStruct(out_shape, jnp.floa...]
where the time goes in v4:
time: 68.2 us; the launch traced here: 68 us
  blocking collectives  37.3 us (55%)
  starting transfers between devices  12.1 us (18%)
  Pallas kernels  12 us (18%)
  waiting for transfers between devices  4.95 us (7%)
  local copies, waits for them, and re-layouts  1.02 us (1%)
  between operations  0.69 us (1%)
    all_to_all x1, blocking collectives, body(): parts = lax.all_to_all(payload, ALL, 0, 0, tiled=True)  19.3 us
    all_to_all x1, blocking collectives, body(): lax.all_to_all(spread(words, 8), 'row', 0, 0, axis_index_groups=cores, ti...  17.9 us
    ppermute x4, starting transfers between devices, body(): lax.ppermute(words, 'col', [((c + t) % 8, c) for c in range(8)])  9.92 us
    pallas_call x2, Pallas kernels, count(): pl.pallas_call(kernel, out_shape=jax.ShapeDtypeStruct(out_shape, jnp.floa...  8.35 us
    ppermute x4, waiting for transfers between devices, body(): lax.ppermute(words, 'col', [((c + t) % 8, c) for c in range(8)])  4.95 us
    pallas_call x2, Pallas kernels, expand(): pl.pallas_call(kernel, out_shape=(jax.ShapeDtypeStruct((len(picks) * dept...  2.82 us
    ppermute x1, starting transfers between devices, body(): oth = lax.ppermute(own, 'row', [(r, r ^ 1) for r in range(16)])  2.19 us
  transfers between devices with their start and end apart: 5, of which 2 were waited for; matrix products, arithmetic and copies ran while one was open for 0% of the time, Pallas kernels for 4%

profile of v4, /device:TPU:1, one launch (start us, length us, event | category | flops | bytes accessed | tf_op | source)
XLA Modules:
  0.0 68.0 jit_solution(7041335473300791996)
XLA Ops:
  0.6 0.0 copy-start
  0.6 1.0 %broadcast_in_dim.4 = s32[8,40,640]{2,1,0:T(8,128)S(1)} broadcast(s32[40,640]{1,0:T(8,128)} %bitcast.4), dimensions={1,2} | broadcast | bytes 921600 | tf_op jit(solution)/shard_map/broadcast_in_dim | solution.py:13
  1.7 17.9 %all_to_all.10.refs_0_ = s32[8,40,640]{2,1,0:T(8,128)S(1)} all-to-all(s32[8,40,640]{2,1,0:T(8,128)S(1)} %broadcast_in_dim.4), channel_id=1, replica_groups={{0,16,32,48,64,80,96,112},{8,24,40,56,72,88,104,120},{1,17,33,49,65,81,..., dimensions={0} | all-to-all | bytes 1638400 | tf_op jit(solution)/shard_map/all_to_all | solution.py:159
  19.6 2.2 %collective-permute-start = (s32[8,40,640]{2,1,0:T(8,128)S(1)}, s32[8,40,640]{2,1,0:T(8,128)S(1)}, u32[]{:S(2)}, u32[]{:S(2)}) collective-permute-start(s32[8,40,640]{2,1,0:T(8,128)S(1)} %all_to_all.10.refs_0_), channel_id=1, source_target_pairs={{0,8},{8,0},{16,24},{24,16},{32,40},{40,32},{48,56},{56,48},{64,72... | collective-permute-start | bytes 2457608 | tf_op jit(solution)/shard_map/ppermute | solution.py:165
  21.8 0.0 copy-done
  21.8 5.9 %collective-permute-start.4 = (s32[40,640]{1,0:T(8,128)S(1)}, s32[40,640]{1,0:T(8,128)S(1)}, u32[]{:S(2)}, u32[]{:S(2)}) collective-permute-start(s32[40,640]{1,0:T(8,128)S(1)} %bitcast.5), channel_id=1, source_target_pairs={{1,0},{2,1},{3,2},{4,3},{5,4},{6,5},{7,6},{0,7},{9,8},{10,9},{11,1... | collective-permute-start | bytes 307208 | tf_op jit(solution)/shard_map/ppermute | solution.py:164
  27.7 0.0 collective-permute-start.3
  27.7 1.5 %collective-permute-start.2 = (s32[40,640]{1,0:T(8,128)S(1)}, s32[40,640]{1,0:T(8,128)S(1)}, u32[]{:S(2)}, u32[]{:S(2)}) collective-permute-start(s32[40,640]{1,0:T(8,128)S(1)} %bitcast.7), channel_id=1, source_target_pairs={{2,0},{3,1},{4,2},{5,3},{6,4},{7,5},{0,6},{1,7},{10,8},{11,9},{12,... | collective-permute-start | bytes 307208 | tf_op jit(solution)/shard_map/ppermute | solution.py:164
  29.3 2.5 %collective-permute-start.1 = (s32[40,640]{1,0:T(8,128)S(1)}, s32[40,640]{1,0:T(8,128)S(1)}, u32[]{:S(2)}, u32[]{:S(2)}) collective-permute-start(s32[40,640]{1,0:T(8,128)S(1)} %bitcast.8), channel_id=1, source_target_pairs={{4,0},{5,1},{6,2},{7,3},{0,4},{1,5},{2,6},{3,7},{12,8},{13,9},{14,... | collective-permute-start | bytes 307208 | tf_op jit(solution)/shard_map/ppermute | solution.py:164
  31.7 0.0 collective-permute-done.4.refs_1_
  31.7 1.1 %shard_map.42 = (f8e4m3fn[2560,640]{1,0:T(32,128)(4,1)S(1)}, f32[1,640]{1,0:T(1,128)S(1)}) custom-call(s32[40,640]{1,0:T(8,128)S(1)} %bitcast.9, s32[40,640]{1,0:T(8,128)S(1)} %collective-permute-done.4.refs_1_), custom_call_target="tpu_custom_call" | custom-call | flops 400000000 | bytes 3000000 | tf_op jit(solution)/shard_map/pallas_call | solution.py:174
  32.8 2.5 %collective-permute-done.3.refs_2_ = s32[40,640]{1,0:T(8,128)S(1)} collective-permute-done((s32[40,640]{1,0:T(8,128)S(1)}, s32[40,640]{1,0:T(8,128)S(1)}, u32[]{:S(2)}, u32[]{:S(2)}) %collective-permute-start.3) | collective-permute-done | bytes 102432 | tf_op jit(solution)/shard_map/ppermute | solution.py:164
  35.3 0.0 collective-permute-done.2.refs_1_
  35.3 2.5 %collective-permute-done.1.refs_0_ = s32[40,640]{1,0:T(8,128)S(1)} collective-permute-done((s32[40,640]{1,0:T(8,128)S(1)}, s32[40,640]{1,0:T(8,128)S(1)}, u32[]{:S(2)}, u32[]{:S(2)}) %collective-permute-start.1) | collective-permute-done | bytes 102432 | tf_op jit(solution)/shard_map/ppermute | solution.py:164
  37.8 1.7 %shard_map.41 = (f8e4m3fn[3840,640]{1,0:T(32,128)(4,1)S(1)}, f32[1,640]{1,0:T(1,128)S(1)}) custom-call(s32[40,640]{1,0:T(8,128)S(1)} %collective-permute-done.1.refs_0_, s32[40,640]{1,0:T(8,128)S(1)} %collective-permute-done.2.refs_1_, s32[40,640]{1,0:T(8,128)S(1)} %collective-permute-done.3.refs_2_), custom_call_target="tpu_custom_call" | custom-call | flops 400000000 | bytes 3000000 | tf_op jit(solution)/shard_map/pallas_call | solution.py:174
  39.5 0.0 collective-permute-done.refs_1_
  39.5 3.2 %shard_map.43.refs_4_ = f32[1280,640]{1,0:T(8,128)S(1)} custom-call(s32[8,40,640]{2,1,0:T(8,128)S(1)} %all_to_all.10.refs_0_, s32[8,40,640]{2,1,0:T(8,128)S(1)} %collective-permute-done.refs_1_, f8e4m3fn[2560,640]{1,0:T(32,128)(4,1)S(1)} %get-tuple-element.9.refs_2_), custom_call_target="tpu_custom_call" | custom-call | flops 4194304000 | bytes 6000000 | tf_op jit(solution)/shard_map/pallas_call | solution.py:196
  42.7 0.0 copy-start.1
  42.7 5.1 %shard_map.44 = f32[128,8,128]{2,1,0:T(8,128)S(1)} custom-call(s32[8,40,640]{2,1,0:T(8,128)S(1)} %all_to_all.10.refs_0_, s32[8,40,640]{2,1,0:T(8,128)S(1)} %collective-permute-done.refs_1_, f8e4m3fn[3840,640]{1,0:T(32,128)(4,1)S(1)} %get-tuple-element.8.refs_2_, s32[40,640]{1,0:T(8,128)S(1)} %bitcast.10, f32[1280,640]{1,0:T(8,128)S(1)} %shard_map.43.refs_4_, ...), custom_call_target="tpu_custom_call" | custom-call | flops 6291456000 | bytes 6000000 | tf_op jit(solution)/shard_map/pallas_call | solution.py:196
  47.9 19.3 %all_to_all.11.parts = f32[128,8,128]{2,1,0:T(8,128)S(1)} all-to-all(f32[128,8,128]{2,1,0:T(8,128)S(1)} %shard_map.44), channel_id=1, replica_groups=mesh['row'=16,'col'=8] {'row','col'}, dimensions={0} | all-to-all | bytes 1048576 | tf_op jit(solution)/shard_map/all_to_all | solution.py:218
  67.2 0.0 copy-done.1
  67.2 0.8 %finish.1 = (f32[1,80]{1,0:T(1,128)}, f32[1,1]{1,0:T(1,128)}) custom-call(f32[128,8,128]{2,1,0:T(8,128)S(1)} %all_to_all.11.parts, s32[1,80]{1,0:T(1,128)S(1)} %bitcast.11), custom_call_target="tpu_custom_call" | custom-call | tf_op jit(solution)/shard_map/finish/pallas_call | solution.py:219
Async XLA Ops:
  0.6 21.2 %copy-start = (s32[640,40]{0,1:T(8,128)S(1)}, s32[640,40]{0,1:T(8,128)}, u32[]{:S(2)}) copy-start(s32[640,40]{0,1:T(8,128)} %param.2) | copy-start | bytes 307204
  19.6 19.9 %collective-permute-start = (s32[8,40,640]{2,1,0:T(8,128)S(1)}, s32[8,40,640]{2,1,0:T(8,128)S(1)}, u32[]{:S(2)}, u32[]{:S(2)}) collective-permute-start(s32[8,40,640]{2,1,0:T(8,128)S(1)} %all_to_all.10.refs_0_), channel_id=1, source_target_pairs={{0,8},{8,0},{16,24},{24,16},{32,40},{40,32},{48,56},{56,48},{64,72... | collective-permute-start | bytes 2457608 | tf_op jit(solution)/shard_map/ppermute | solution.py:165
  21.8 9.9 %collective-permute-start.4 = (s32[40,640]{1,0:T(8,128)S(1)}, s32[40,640]{1,0:T(8,128)S(1)}, u32[]{:S(2)}, u32[]{:S(2)}) collective-permute-start(s32[40,640]{1,0:T(8,128)S(1)} %bitcast.5), channel_id=1, source_target_pairs={{1,0},{2,1},{3,2},{4,3},{5,4},{6,5},{7,6},{0,7},{9,8},{10,9},{11,1... | collective-permute-start | bytes 307208 | tf_op jit(solution)/shard_map/ppermute | solution.py:164
  27.7 7.6 %collective-permute-start.3 = (s32[40,640]{1,0:T(8,128)S(1)}, s32[40,640]{1,0:T(8,128)S(1)}, u32[]{:S(2)}, u32[]{:S(2)}) collective-permute-start(s32[40,640]{1,0:T(8,128)S(1)} %bitcast.6), channel_id=1, source_target_pairs={{3,0},{4,1},{5,2},{6,3},{7,4},{0,5},{1,6},{2,7},{11,8},{12,9},{13,... | collective-permute-start | bytes 307208 | tf_op jit(solution)/shard_map/ppermute | solution.py:164
  27.7 7.6 %collective-permute-start.2 = (s32[40,640]{1,0:T(8,128)S(1)}, s32[40,640]{1,0:T(8,128)S(1)}, u32[]{:S(2)}, u32[]{:S(2)}) collective-permute-start(s32[40,640]{1,0:T(8,128)S(1)} %bitcast.7), channel_id=1, source_target_pairs={{2,0},{3,1},{4,2},{5,3},{6,4},{7,5},{0,6},{1,7},{10,8},{11,9},{12,... | collective-permute-start | bytes 307208 | tf_op jit(solution)/shard_map/ppermute | solution.py:164
  29.3 8.5 %collective-permute-start.1 = (s32[40,640]{1,0:T(8,128)S(1)}, s32[40,640]{1,0:T(8,128)S(1)}, u32[]{:S(2)}, u32[]{:S(2)}) collective-permute-start(s32[40,640]{1,0:T(8,128)S(1)} %bitcast.8), channel_id=1, source_target_pairs={{4,0},{5,1},{6,2},{7,3},{0,4},{1,5},{2,6},{3,7},{12,8},{13,9},{14,... | collective-permute-start | bytes 307208 | tf_op jit(solution)/shard_map/ppermute | solution.py:164
  42.7 24.5 %copy-start.1 = (s32[80]{0:T(128)S(1)}, s32[80]{0:T(128)}, u32[]{:S(2)}) copy-start(s32[80]{0:T(128)} %param.3) | copy-start | bytes 964

commit v5 on v3

v5 whole, which is shorter than its diff:
```python
import jax
import jax.numpy as jnp
from jax import lax
from jax.experimental import pallas as pl
from jax.experimental.pallas import tpu as pltpu
from jax.sharding import PartitionSpec as P

ALL = ("row", "col")
WINDOW = 5


def spread(value, peers):
    return jnp.broadcast_to(value[None], (peers, *value.shape))


def shifted(row, step):
    words = jnp.broadcast_to(row, (32, row.shape[1]))
    return lax.shift_right_logical(words, step)


def weighted(row, weight, dtype):
    bit = lax.broadcasted_iota(jnp.int32, (32, row.shape[1]), 0)
    value = (shifted(row, bit).astype(jnp.int8) & jnp.int8(1)).astype(jnp.bfloat16)
    return (value * weight if weight != 1 else value).astype(dtype)


FIRST = (((0, 0), (0, 2)),)
REST = (((1, 0), (1, 2)), ((0, 4), (1, 4)), ((0, 1), (1, 1)), ((0, 3), (1, 3)))
WEIGHTS = (1, 2, 2, 2, 1)


TILE = 256


def fill_right(target, rows, step, tile, core):
    half = 20
    for w in range(8 * tile, 8 * tile + 8):
        side, t = step[w // half]
        base = half * (core if side == 0 else 1 - core) + w % half
        target[w * 32 : w * 32 + 32, :] = weighted(
            rows[t][pl.ds(base, 1), :], WEIGHTS[t], target.dtype
        )


def fill_left(target, sources, step, tile, places):
    for k, (side, t) in enumerate(step):
        words = sources[side][places[t], 8 * tile : 8 * tile + 8, :]
        octets = jnp.concatenate(
            [lax.shift_right_logical(words, jnp.int32(8 * byte)) for byte in range(4)], axis=0
        ).astype(jnp.int8)
        for s in range(8):
            picked = octets & jnp.int8(-128 if s == 7 else 1 << s)
            at = tile * TILE + s * 32
            target[at : at + 32, k * 640 : k * 640 + 640] = picked.astype(
                jnp.bfloat16
            ).astype(target.dtype)


def label_of(col):
    return (col % 4) * 2 + col // 4


def place_of(label):
    return (label % 2) * 4 + (label % 8) // 2


def places_of(col):
    return [place_of(label_of(col) + t) for t in range(WINDOW)]


def early_kernel(r2, right):
    core = lax.rem(lax.axis_index("row"), 2)
    for w in range(20):
        right[w * 32 : w * 32 + 32, :] = weighted(
            r2[pl.ds(20 * core + w, 1), :], WEIGHTS[2], right.dtype
        )


def product(left, right, tile):
    return jnp.dot(
        left[tile * TILE : tile * TILE + TILE, :],
        right[...],
        preferred_element_type=jnp.float32,
    )


def begin_kernel(own, early, paths, left, right):
    chip = lax.axis_index("row") // 2
    core = lax.rem(lax.axis_index("row"), 2)
    places = places_of(lax.axis_index("col"))
    right[640:, :] = early[...]
    for w in range(20):
        right[w * 32 : w * 32 + 32, :] = weighted(
            own[chip, pl.ds(20 * core + w, 1), :], WEIGHTS[0], right.dtype
        )
    fill_left(left, (own,), FIRST[0], 0, places)
    for tile in range(5):
        if tile < 4:
            fill_left(left, (own,), FIRST[0], tile + 1, places)
        paths[tile * TILE : tile * TILE + TILE, :] = product(left, right, tile)


def count_kernel(own, oth, r1, r2, r3, r4, paths, out, la, lb, ra, rb, acc):
    chip = lax.axis_index("row") // 2
    core = lax.rem(lax.axis_index("row"), 2)
    col = lax.axis_index("col")
    places = places_of(col)
    mask = own.at[chip]
    rows = (mask, r1, r2, r3, r4)
    lanes = r1.shape[1]
    left, right = (la, lb), (ra, rb)
    for tile in range(5):
        fill_left(la, (own, oth), REST[0], tile, places)
        fill_right(ra, rows, REST[0], tile, core)
    total = jnp.zeros((8, lanes), jnp.float32)
    for k in range(len(REST)):
        now, later = k % 2, (k + 1) % 2
        known = paths if k == 0 else acc
        for tile in range(5):
            if k + 1 < len(REST):
                fill_left(left[later], (own, oth), REST[k + 1], tile, places)
                fill_right(right[later], rows, REST[k + 1], tile, core)
            piece = slice(tile * TILE, tile * TILE + TILE)
            value = known[piece, :] + product(left[now], right[now], tile)
            if k + 1 < len(REST):
                acc[piece, :] = value
                continue
            words = mask[8 * tile : 8 * tile + 8, :]
            for s in range(8):
                part = 0.0
                for byte in range(4):
                    at = s * 32 + byte * 8
                    spot = 8 * byte + s
                    hit = (words & jnp.int32(-(2**31) if spot == 31 else 1 << spot)) != 0
                    part = part + jnp.where(hit, value[at : at + 8, :], 0.0)
                total = total + part * (-(2.0**-7) if s == 7 else 2.0**-s)
    closed = jnp.sum(total, axis=0, keepdims=True)
    links = sum(lax.population_count(rows[t][...]) for t in range(4))
    degree = jnp.sum(links, axis=0, keepdims=True).astype(jnp.float32)
    part = label_of(col) % 4
    first = jnp.where(
        part == 0,
        degree[:, :128],
        jnp.where(part == 1, degree[:, 256:384], degree[:, 512:]),
    )
    second = jnp.where(part == 0, degree[:, 128:256], degree[:, 384:512])
    payload = jnp.concatenate(
        [closed[:, 128 * j : 128 * j + 128] for j in range(5)] + [first, second, first],
        axis=0,
    )
    out[...] = jnp.broadcast_to(payload[None], out.shape)


def finish_kernel(parts, relabel, clustering, transitivity):
    value = parts[...].reshape(16, 8, 8, 128)
    closed = value[:, :, :5].sum(axis=1)
    slots = [value[:, place_of(m), 5:7] + value[:, place_of(m + 4), 5:7] for m in range(3)]
    degree = jnp.concatenate([slots[0], slots[1], slots[2][:, :1]], axis=1)
    wedges = jnp.maximum(degree * (degree - 1.0), 1.0)
    ratio = (closed / wedges).reshape(80, 128)
    index = relabel[...]
    line = index // 128
    lane = index - line * 128
    hot = (lax.broadcasted_iota(jnp.int32, (128, 80), 0) == lane).astype(jnp.float32)
    picked = jnp.dot(
        ratio, hot, preferred_element_type=jnp.float32, precision=lax.Precision.HIGHEST
    )
    mine = lax.broadcasted_iota(jnp.int32, (80, 80), 0) == line
    clustering[...] = jnp.sum(jnp.where(mine, picked, 0.0), axis=0, keepdims=True)
    total = jnp.sum(closed.reshape(80, 128), axis=0, keepdims=True)
    pairs = jnp.sum(wedges.reshape(80, 128), axis=0, keepdims=True)
    transitivity[...] = jnp.sum(total, axis=1, keepdims=True) / jnp.sum(
        pairs, axis=1, keepdims=True
    )


def body(adjacency, relabel, dtype=jnp.float8_e4m3fn):
    words = adjacency.T
    cores = [[2 * chip + core for chip in range(8)] for core in range(2)]
    own = lax.all_to_all(
        spread(words, 8), "row", 0, 0, axis_index_groups=cores, tiled=True
    )
    rows = [words]
    for t in range(1, WINDOW):
        rows.append(
            lax.ppermute(
                words, "col", [(place_of(label_of(c) + t), c) for c in range(8)]
            )
        )
    oth = lax.ppermute(own, "row", [(r, r ^ 1) for r in range(16)])
    vmem = pl.BlockSpec(memory_space=pltpu.VMEM)
    depth = words.shape[0] * 32
    lanes = words.shape[1]
    left = pltpu.VMEM((depth, depth), dtype)
    right = pltpu.VMEM((depth, lanes), dtype)
    acc = pltpu.VMEM((depth, lanes), jnp.float32)

    def call(kernel, operands, out_shape, scratch, steps, mib):
        return pl.pallas_call(
            kernel,
            out_shape=out_shape,
            in_specs=[vmem] * len(operands),
            out_specs=vmem,
            scratch_shapes=scratch,
            compiler_params=pltpu.CompilerParams(vmem_limit_bytes=mib * 2**20),
            cost_estimate=pl.CostEstimate(
                flops=max(2 * steps * depth * depth * lanes, 10**8),
                bytes_accessed=5 * 10**6,
                transcendentals=0,
            ),
        )(*operands)

    early = call(
        early_kernel,
        rows[2:3],
        jax.ShapeDtypeStruct((depth // 2, lanes), dtype),
        [],
        0,
        4,
    )
    paths = call(
        begin_kernel,
        (own, early),
        jax.ShapeDtypeStruct((depth, lanes), jnp.float32),
        [left, right],
        len(FIRST),
        16,
    )
    payload = call(
        count_kernel,
        (own, oth, *rows[1:], paths),
        jax.ShapeDtypeStruct((128, 8, 128), jnp.float32),
        [left, left, right, right, acc],
        len(REST),
        24,
    )
    parts = lax.all_to_all(payload, ALL, 0, 0, tiled=True)
    clustering, transitivity = pl.pallas_call(
        finish_kernel,
        out_shape=(
            jax.ShapeDtypeStruct((1, 80), jnp.float32),
            jax.ShapeDtypeStruct((1, 1), jnp.float32),
        ),
        in_specs=[vmem] * 2,
        out_specs=(vmem, vmem),
        compiler_params=pltpu.CompilerParams(vmem_limit_bytes=4 * 2**20),
        name="finish",
    )(parts, relabel[None])
    return clustering[0], transitivity[0, 0]


def solution(mesh):
    return jax.shard_map(
        body,
        mesh=mesh,
        in_specs=(P("row", "col"), P(ALL)),
        out_specs=(P(ALL), P()),
        check_vma=False,
    )
```

time: 69.3 us -> 64.7 us (0.934)
  Pallas kernels: 13 us -> 8.92 us
  blocking collectives: 37.4 us -> 39.4 us
  waiting for transfers between devices: 4.95 us -> 2.99 us
    pallas_call x3, Pallas kernels: 11.1 us -> 8.1 us  [call(): pl.pallas_call(kernel, out_shape=out_shape, in_specs=[vmem] * len(operand...]
    all_to_all x1, blocking collectives: 19.4 us -> 21.4 us  [body(): parts = lax.all_to_all(payload, ALL, 0, 0, tiled=True)]
    ppermute x4, waiting for transfers between devices: 4.95 us -> 2.99 us  [body(): lax.ppermute(words, 'col', [(place_of(label_of(c) + t), c) for c in range...]
    pallas_call x1, Pallas kernels: 1.86 us -> 0.81 us  [body(): pl.pallas_call(finish_kernel, out_shape=(jax.ShapeDtypeStruct((1, 80), jn...]
  transfers between devices with their start and end apart: 5 -> 5, of which waited for: 2 -> 2; matrix products, arithmetic and copies ran while one was open for 0% -> 0% of each run, Pallas kernels for 4% -> 3%
where the time goes in v5:
time: 64.7 us; the launch traced here: 64.5 us
  blocking collectives  39.4 us (61%)
  starting transfers between devices  11.6 us (18%)
  Pallas kernels  8.92 us (14%)
  waiting for transfers between devices  2.99 us (5%)
  local copies, waits for them, and re-layouts  0.96 us (1%)
  between operations  0.68 us (1%)
    all_to_all x1, blocking collectives, body(): parts = lax.all_to_all(payload, ALL, 0, 0, tiled=True)  21.4 us
    all_to_all x1, blocking collectives, body(): lax.all_to_all(spread(words, 8), 'row', 0, 0, axis_index_groups=cores, ti...  17.9 us
    ppermute x4, starting transfers between devices, body(): lax.ppermute(words, 'col', [(place_of(label_of(c) + t), c) for c in range...  9.41 us
    pallas_call x3, Pallas kernels, call(): pl.pallas_call(kernel, out_shape=out_shape, in_specs=[vmem] * len(operand...  8.1 us
    ppermute x4, waiting for transfers between devices, body(): lax.ppermute(words, 'col', [(place_of(label_of(c) + t), c) for c in range...  2.99 us
    ppermute x1, starting transfers between devices, body(): oth = lax.ppermute(own, 'row', [(r, r ^ 1) for r in range(16)])  2.19 us
  transfers between devices with their start and end apart: 5, of which 2 were waited for; matrix products, arithmetic and copies ran while one was open for 0% of the time, Pallas kernels for 3%

profile of v5, /device:TPU:1, one launch (start us, length us, event | category | flops | bytes accessed | tf_op | source)
XLA Modules:
  0.0 64.5 jit_solution(6660843459456887255)
XLA Ops:
  0.6 0.9 %broadcast_in_dim.4 = s32[8,40,640]{2,1,0:T(8,128)S(1)} broadcast(s32[40,640]{1,0:T(8,128)} %bitcast.5), dimensions={1,2} | broadcast | bytes 921600 | tf_op jit(solution)/shard_map/broadcast_in_dim | solution.py:13
  1.6 17.9 %all_to_all.10.own = s32[8,40,640]{2,1,0:T(8,128)S(1)} all-to-all(s32[8,40,640]{2,1,0:T(8,128)S(1)} %broadcast_in_dim.4), channel_id=1, replica_groups={{0,16,32,48,64,80,96,112},{8,24,40,56,72,88,104,120},{1,17,33,49,65,81,..., dimensions={0} | all-to-all | bytes 1638400 | tf_op jit(solution)/shard_map/all_to_all | solution.py:180
  19.5 2.2 %collective-permute-start = (s32[8,40,640]{2,1,0:T(8,128)S(1)}, s32[8,40,640]{2,1,0:T(8,128)S(1)}, u32[]{:S(2)}, u32[]{:S(2)}) collective-permute-start(s32[8,40,640]{2,1,0:T(8,128)S(1)} %all_to_all.10.own), channel_id=1, source_target_pairs={{0,8},{8,0},{16,24},{24,16},{32,40},{40,32},{48,56},{56,48},{64,72... | collective-permute-start | bytes 2457608 | tf_op jit(solution)/shard_map/ppermute | solution.py:190
  21.7 3.8 %collective-permute-start.2 = (s32[40,640]{1,0:T(8,128)}, s32[40,640]{1,0:T(8,128)S(1)}, u32[]{:S(2)}, u32[]{:S(2)}) collective-permute-start(s32[40,640]{1,0:T(8,128)} %bitcast.6), channel_id=1, source_target_pairs={{1,0},{2,1},{3,2},{0,3},{5,4},{6,5},{7,6},{4,7},{9,8},{10,9},{11,1... | collective-permute-start | bytes 307208 | tf_op jit(solution)/shard_map/ppermute | solution.py:186
  25.5 0.0 collective-permute-start.4
  25.5 5.1 %collective-permute-start.3 = (s32[40,640]{1,0:T(8,128)}, s32[40,640]{1,0:T(8,128)S(1)}, u32[]{:S(2)}, u32[]{:S(2)}) collective-permute-start(s32[40,640]{1,0:T(8,128)} %bitcast.8), channel_id=1, source_target_pairs={{5,0},{6,1},{7,2},{4,3},{2,4},{3,5},{0,6},{1,7},{13,8},{14,9},{15,... | collective-permute-start | bytes 307208 | tf_op jit(solution)/shard_map/ppermute | solution.py:186
  30.6 0.5 collective-permute-start.1
  31.1 1.2 %collective-permute-done.2.r2 = s32[40,640]{1,0:T(8,128)S(1)} collective-permute-done((s32[40,640]{1,0:T(8,128)}, s32[40,640]{1,0:T(8,128)S(1)}, u32[]{:S(2)}, u32[]{:S(2)}) %collective-permute-start.2) | collective-permute-done | bytes 102432 | tf_op jit(solution)/shard_map/ppermute | solution.py:186
  32.3 0.2 shard_map.41.early
  32.5 1.5 %shard_map.42.paths = f32[1280,640]{1,0:T(8,128)S(1)} custom-call(s32[8,40,640]{2,1,0:T(8,128)S(1)} %all_to_all.10.own, f8e4m3fn[640,640]{1,0:T(32,128)(4,1)S(1)} %shard_map.41.early), custom_call_target="tpu_custom_call" | custom-call | flops 2097152000 | bytes 5000000 | tf_op jit(solution)/shard_map/pallas_call | solution.py:199
  34.0 0.0 copy-start
  34.0 0.0 collective-permute-done.4.r4
  34.0 0.0 collective-permute-done.3.r3
  34.0 1.8 %collective-permute-done.1.r1 = s32[40,640]{1,0:T(8,128)S(1)} collective-permute-done((s32[40,640]{1,0:T(8,128)}, s32[40,640]{1,0:T(8,128)S(1)}, u32[]{:S(2)}, u32[]{:S(2)}) %collective-permute-start.1) | collective-permute-done | bytes 102432 | tf_op jit(solution)/shard_map/ppermute | solution.py:186
  35.8 0.0 collective-permute-done.oth
  35.8 6.4 %shard_map.43 = f32[128,8,128]{2,1,0:T(8,128)S(1)} custom-call(s32[8,40,640]{2,1,0:T(8,128)S(1)} %all_to_all.10.own, s32[8,40,640]{2,1,0:T(8,128)S(1)} %collective-permute-done.oth, s32[40,640]{1,0:T(8,128)S(1)} %collective-permute-done.1.r1, s32[40,640]{1,0:T(8,128)S(1)} %collective-permute-done.2.r2, s32[40,640]{1,0:T(8,128)S(1)} %collective-permute-done.3.r3, ...), custom_call_target="tpu_custom_call" | custom-call | flops 8388608000 | bytes 5000000 | tf_op jit(solution)/shard_map/pallas_call | solution.py:199
  42.3 21.4 %all_to_all.11.parts = f32[128,8,128]{2,1,0:T(8,128)S(1)} all-to-all(f32[128,8,128]{2,1,0:T(8,128)S(1)} %shard_map.43), channel_id=1, replica_groups=mesh['row'=16,'col'=8] {'row','col'}, dimensions={0} | all-to-all | bytes 1048576 | tf_op jit(solution)/shard_map/all_to_all | solution.py:237
  63.7 0.0 copy-done
  63.7 0.8 %finish.1 = (f32[1,80]{1,0:T(1,128)}, f32[1,1]{1,0:T(1,128)}) custom-call(f32[128,8,128]{2,1,0:T(8,128)S(1)} %all_to_all.11.parts, s32[1,80]{1,0:T(1,128)S(1)} %bitcast.4), custom_call_target="tpu_custom_call" | custom-call | tf_op jit(solution)/shard_map/finish/pallas_call | solution.py:238
Async XLA Ops:
  19.5 16.3 %collective-permute-start = (s32[8,40,640]{2,1,0:T(8,128)S(1)}, s32[8,40,640]{2,1,0:T(8,128)S(1)}, u32[]{:S(2)}, u32[]{:S(2)}) collective-permute-start(s32[8,40,640]{2,1,0:T(8,128)S(1)} %all_to_all.10.own), channel_id=1, source_target_pairs={{0,8},{8,0},{16,24},{24,16},{32,40},{40,32},{48,56},{56,48},{64,72... | collective-permute-start | bytes 2457608 | tf_op jit(solution)/shard_map/ppermute | solution.py:190
  21.7 10.6 %collective-permute-start.2 = (s32[40,640]{1,0:T(8,128)}, s32[40,640]{1,0:T(8,128)S(1)}, u32[]{:S(2)}, u32[]{:S(2)}) collective-permute-start(s32[40,640]{1,0:T(8,128)} %bitcast.6), channel_id=1, source_target_pairs={{1,0},{2,1},{3,2},{0,3},{5,4},{6,5},{7,6},{4,7},{9,8},{10,9},{11,1... | collective-permute-start | bytes 307208 | tf_op jit(solution)/shard_map/ppermute | solution.py:186
  25.5 8.5 %collective-permute-start.4 = (s32[40,640]{1,0:T(8,128)}, s32[40,640]{1,0:T(8,128)S(1)}, u32[]{:S(2)}, u32[]{:S(2)}) collective-permute-start(s32[40,640]{1,0:T(8,128)} %bitcast.7), channel_id=1, source_target_pairs={{2,0},{3,1},{0,2},{1,3},{6,4},{7,5},{4,6},{5,7},{10,8},{11,9},{8,1... | collective-permute-start | bytes 307208 | tf_op jit(solution)/shard_map/ppermute | solution.py:186
  25.5 8.5 %collective-permute-start.3 = (s32[40,640]{1,0:T(8,128)}, s32[40,640]{1,0:T(8,128)S(1)}, u32[]{:S(2)}, u32[]{:S(2)}) collective-permute-start(s32[40,640]{1,0:T(8,128)} %bitcast.8), channel_id=1, source_target_pairs={{5,0},{6,1},{7,2},{4,3},{2,4},{3,5},{0,6},{1,7},{13,8},{14,9},{15,... | collective-permute-start | bytes 307208 | tf_op jit(solution)/shard_map/ppermute | solution.py:186
  30.6 5.2 %collective-permute-start.1 = (s32[40,640]{1,0:T(8,128)}, s32[40,640]{1,0:T(8,128)S(1)}, u32[]{:S(2)}, u32[]{:S(2)}) collective-permute-start(s32[40,640]{1,0:T(8,128)} %bitcast.9), channel_id=1, source_target_pairs={{4,0},{5,1},{6,2},{7,3},{1,4},{2,5},{3,6},{0,7},{12,8},{13,9},{14,... | collective-permute-start | bytes 307208 | tf_op jit(solution)/shard_map/ppermute | solution.py:186
  34.0 29.7 %copy-start = (s32[80]{0:T(128)S(1)}, s32[80]{0:T(128)}, u32[]{:S(2)}) copy-start(s32[80]{0:T(128)} %param.3) | copy-start | bytes 964

commit v6 on v5

--- a/solution.py
+++ b/solution.py
@@ -68,12 +68,12 @@
     return [place_of(label_of(col) + t) for t in range(WINDOW)]
 
 
-def early_kernel(r2, right):
+def early_kernel(r0, r2, right_first, right_next):
     core = lax.rem(lax.axis_index("row"), 2)
-    for w in range(20):
-        right[w * 32 : w * 32 + 32, :] = weighted(
-            r2[pl.ds(20 * core + w, 1), :], WEIGHTS[2], right.dtype
-        )
+    rows = (r0, None, r2)
+    for tile in range(5):
+        fill_right(right_first, rows, FIRST[0], tile, core)
+        fill_right(right_next, rows, REST[0], tile, core)
 
 
 def product(left, right, tile):
@@ -84,15 +84,8 @@
     )
 
 
-def begin_kernel(own, early, paths, left, right):
-    chip = lax.axis_index("row") // 2
-    core = lax.rem(lax.axis_index("row"), 2)
+def begin_kernel(own, right, paths, left):
     places = places_of(lax.axis_index("col"))
-    right[640:, :] = early[...]
-    for w in range(20):
-        right[w * 32 : w * 32 + 32, :] = weighted(
-            own[chip, pl.ds(20 * core + w, 1), :], WEIGHTS[0], right.dtype
-        )
     fill_left(left, (own,), FIRST[0], 0, places)
     for tile in range(5):
         if tile < 4:
@@ -100,7 +93,7 @@
         paths[tile * TILE : tile * TILE + TILE, :] = product(left, right, tile)
 
 
-def count_kernel(own, oth, r1, r2, r3, r4, paths, out, la, lb, ra, rb, acc):
+def count_kernel(own, oth, r1, r2, r3, r4, right_next, paths, out, la, lb, ra, rb, acc):
     chip = lax.axis_index("row") // 2
     core = lax.rem(lax.axis_index("row"), 2)
     col = lax.axis_index("col")
@@ -111,7 +104,6 @@
     left, right = (la, lb), (ra, rb)
     for tile in range(5):
         fill_left(la, (own, oth), REST[0], tile, places)
-        fill_right(ra, rows, REST[0], tile, core)
     total = jnp.zeros((8, lanes), jnp.float32)
     for k in range(len(REST)):
         now, later = k % 2, (k + 1) % 2
@@ -121,7 +113,8 @@
                 fill_left(left[later], (own, oth), REST[k + 1], tile, places)
                 fill_right(right[later], rows, REST[k + 1], tile, core)
             piece = slice(tile * TILE, tile * TILE + TILE)
-            value = known[piece, :] + product(left[now], right[now], tile)
+            factor = right_next if k == 0 else right[now]
+            value = known[piece, :] + product(left[now], factor, tile)
             if k + 1 < len(REST):
                 acc[piece, :] = value
                 continue
@@ -151,11 +144,24 @@
     out[...] = jnp.broadcast_to(payload[None], out.shape)
 
 
-def finish_kernel(parts, relabel, clustering, transitivity):
-    value = parts[...].reshape(16, 8, 8, 128)
+def reduced(parts):
+    value = parts[...].reshape(8, 8, 8, 128)
     closed = value[:, :, :5].sum(axis=1)
     slots = [value[:, place_of(m), 5:7] + value[:, place_of(m + 4), 5:7] for m in range(3)]
-    degree = jnp.concatenate([slots[0], slots[1], slots[2][:, :1]], axis=1)
+    return closed, jnp.concatenate([slots[0], slots[1], slots[2][:, :1]], axis=1)
+
+
+def interleaved(mine, other, core):
+    first = jnp.where(core == 0, mine, other)
+    second = jnp.where(core == 0, other, mine)
+    return jnp.stack([first, second], axis=1).reshape(16, 5, 128)
+
+
+def finish_kernel(own, oth, relabel, clustering, transitivity):
+    core = lax.rem(lax.axis_index("row"), 2)
+    closed, degree = (
+        interleaved(mine, other, core) for mine, other in zip(reduced(own), reduced(oth))
+    )
     wedges = jnp.maximum(degree * (degree - 1.0), 1.0)
     ratio = (closed / wedges).reshape(80, 128)
     index = relabel[...]
@@ -200,7 +206,7 @@
             kernel,
             out_shape=out_shape,
             in_specs=[vmem] * len(operands),
-            out_specs=vmem,
+            out_specs=jax.tree.map(lambda _: vmem, out_shape),
             scratch_shapes=scratch,
             compiler_params=pltpu.CompilerParams(vmem_limit_bytes=mib * 2**20),
             cost_estimate=pl.CostEstimate(
@@ -210,42 +216,43 @@
             ),
         )(*operands)
 
-    early = call(
-        early_kernel,
-        rows[2:3],
-        jax.ShapeDtypeStruct((depth // 2, lanes), dtype),
-        [],
-        0,
-        4,
+    operand = jax.ShapeDtypeStruct((depth, lanes), dtype)
+    right_first, right_next = call(
+        early_kernel, (rows[0], rows[2]), (operand, operand), [], 0, 8
     )
     paths = call(
         begin_kernel,
-        (own, early),
+        (own, right_first),
         jax.ShapeDtypeStruct((depth, lanes), jnp.float32),
-        [left, right],
+        [left],
         len(FIRST),
         16,
     )
     payload = call(
         count_kernel,
-        (own, oth, *rows[1:], paths),
-        jax.ShapeDtypeStruct((128, 8, 128), jnp.float32),
+        (own, oth, *rows[1:], right_next, paths),
+        jax.ShapeDtypeStruct((64, 8, 128), jnp.float32),
         [left, left, right, right, acc],
         len(REST),
         24,
     )
-    parts = lax.all_to_all(payload, ALL, 0, 0, tiled=True)
+    peers = [
+        [(2 * chip + core) * 8 + c for chip in range(8) for c in range(8)]
+        for core in range(2)
+    ]
+    parts = lax.all_to_all(payload, ALL, 0, 0, axis_index_groups=peers, tiled=True)
+    across = lax.ppermute(parts, "row", [(r, r ^ 1) for r in range(16)])
     clustering, transitivity = pl.pallas_call(
         finish_kernel,
         out_shape=(
             jax.ShapeDtypeStruct((1, 80), jnp.float32),
             jax.ShapeDtypeStruct((1, 1), jnp.float32),
         ),
-        in_specs=[vmem] * 2,
+        in_specs=[vmem] * 3,
         out_specs=(vmem, vmem),
         compiler_params=pltpu.CompilerParams(vmem_limit_bytes=4 * 2**20),
         name="finish",
-    )(parts, relabel[None])
+    )(parts, across, relabel[None])
     return clustering[0], transitivity[0, 0]
 
 

time: 64.7 us -> 64.4 us (level)
  starting transfers between devices: 11.6 us -> 13.7 us
  blocking collectives: 39.4 us -> 37.5 us
  waiting for transfers between devices: 2.99 us -> 1.29 us
  local copies, waits for them, and re-layouts: 0.96 us -> 1.88 us
    ppermute x4, waiting for transfers between devices: 2.99 us -> 0.12 us  [body(): lax.ppermute(words, 'col', [(place_of(label_of(c) + t), c) for c in range...]
    ppermute x0 -> x1, starting transfers between devices: none -> 2.07 us  [body(): across = lax.ppermute(parts, 'row', [(r, r ^ 1) for r in range(16)])]
    all_to_all x1, blocking collectives: 21.4 us -> 19.6 us  [body(): lax.all_to_all(payload, ALL, 0, 0, axis_index_groups=peers, tiled=True)]
    ppermute x0 -> x1, waiting for transfers between devices: none -> 1.16 us  [body(): across = lax.ppermute(parts, 'row', [(r, r ^ 1) for r in range(16)])]
    unnamed x2 -> x4, local copies, waits for them, and re-layouts: 0.01 us -> 0.93 us
  transfers between devices with their start and end apart: 5 -> 6, of which waited for: 2 -> 2; matrix products, arithmetic and copies ran while one was open for 0% -> 0% of each run, Pallas kernels for 3% -> 3%
where the time goes in v6:
time: 64.4 us; the launch traced here: 64.1 us
  blocking collectives  37.5 us (58%)
  starting transfers between devices  13.7 us (21%)
  Pallas kernels  9.09 us (14%)
  local copies, waits for them, and re-layouts  1.88 us (3%)
  waiting for transfers between devices  1.29 us (2%)
  between operations  0.67 us (1%)
    all_to_all x1, blocking collectives, body(): lax.all_to_all(payload, ALL, 0, 0, axis_index_groups=peers, tiled=True)  19.6 us
    all_to_all x1, blocking collectives, body(): lax.all_to_all(spread(words, 8), 'row', 0, 0, axis_index_groups=cores, ti...  17.9 us
    ppermute x4, starting transfers between devices, body(): lax.ppermute(words, 'col', [(place_of(label_of(c) + t), c) for c in range...  9.41 us
    pallas_call x3, Pallas kernels, call(): pl.pallas_call(kernel, out_shape=out_shape, in_specs=[vmem] * len(operand...  8.27 us
    ppermute x1, starting transfers between devices, body(): oth = lax.ppermute(own, 'row', [(r, r ^ 1) for r in range(16)])  2.19 us
    ppermute x1, starting transfers between devices, body(): across = lax.ppermute(parts, 'row', [(r, r ^ 1) for r in range(16)])  2.07 us
  transfers between devices with their start and end apart: 6, of which 2 were waited for; matrix products, arithmetic and copies ran while one was open for 0% of the time, Pallas kernels for 3%

profile of v6, /device:TPU:1, one launch (start us, length us, event | category | flops | bytes accessed | tf_op | source)
XLA Modules:
  0.0 64.1 jit_solution(12549061356623036234)
XLA Ops:
  0.6 0.9 %broadcast_in_dim.4 = s32[8,40,640]{2,1,0:T(8,128)S(1)} broadcast(s32[40,640]{1,0:T(8,128)} %bitcast.4), dimensions={1,2} | broadcast | bytes 921600 | tf_op jit(solution)/shard_map/broadcast_in_dim | solution.py:13
  1.6 17.9 %all_to_all.10.own = s32[8,40,640]{2,1,0:T(8,128)S(1)} all-to-all(s32[8,40,640]{2,1,0:T(8,128)S(1)} %broadcast_in_dim.4), channel_id=1, replica_groups={{0,16,32,48,64,80,96,112},{8,24,40,56,72,88,104,120},{1,17,33,49,65,81,..., dimensions={0} | all-to-all | bytes 1638400 | tf_op jit(solution)/shard_map/all_to_all | solution.py:186
  19.5 2.2 %collective-permute-start = (s32[8,40,640]{2,1,0:T(8,128)S(1)}, s32[8,40,640]{2,1,0:T(8,128)S(1)}, u32[]{:S(2)}, u32[]{:S(2)}) collective-permute-start(s32[8,40,640]{2,1,0:T(8,128)S(1)} %all_to_all.10.own), channel_id=1, source_target_pairs={{0,8},{8,0},{16,24},{24,16},{32,40},{40,32},{48,56},{56,48},{64,72... | collective-permute-start | bytes 2457608 | tf_op jit(solution)/shard_map/ppermute | solution.py:196
  21.7 3.8 %collective-permute-start.2 = (s32[40,640]{1,0:T(8,128)}, s32[40,640]{1,0:T(8,128)S(1)}, u32[]{:S(2)}, u32[]{:S(2)}) collective-permute-start(s32[40,640]{1,0:T(8,128)} %bitcast.5), channel_id=1, source_target_pairs={{1,0},{2,1},{3,2},{0,3},{5,4},{6,5},{7,6},{4,7},{9,8},{10,9},{11,1... | collective-permute-start | bytes 307208 | tf_op jit(solution)/shard_map/ppermute | solution.py:192
  25.5 2.3 %collective-permute-start.1 = (s32[40,640]{1,0:T(8,128)}, s32[40,640]{1,0:T(8,128)S(1)}, u32[]{:S(2)}, u32[]{:S(2)}) collective-permute-start(s32[40,640]{1,0:T(8,128)} %bitcast.6), channel_id=1, source_target_pairs={{4,0},{5,1},{6,2},{7,3},{1,4},{2,5},{3,6},{0,7},{12,8},{13,9},{14,... | collective-permute-start | bytes 307208 | tf_op jit(solution)/shard_map/ppermute | solution.py:192
  27.8 0.2 collective-permute-start.3
  28.0 3.1 %collective-permute-start.4 = (s32[40,640]{1,0:T(8,128)}, s32[40,640]{1,0:T(8,128)S(1)}, u32[]{:S(2)}, u32[]{:S(2)}) collective-permute-start(s32[40,640]{1,0:T(8,128)} %bitcast.8), channel_id=1, source_target_pairs={{2,0},{3,1},{0,2},{1,3},{6,4},{7,5},{4,6},{5,7},{10,8},{11,9},{8,1... | collective-permute-start | bytes 307208 | tf_op jit(solution)/shard_map/ppermute | solution.py:192
  31.1 0.0 collective-permute-done.2.r2
  31.1 0.0 copy-start
  31.1 0.9 %copy-done = s32[640,40]{0,1:T(8,128)S(1)} copy-done((s32[640,40]{0,1:T(8,128)S(1)}, s32[640,40]{0,1:T(8,128)}, u32[]{:S(2)}) %copy-start) | copy-done | bytes 102424
  32.1 0.7 %shard_map.41 = (f8e4m3fn[1280,640]{1,0:T(32,128)(4,1)S(1)}, f8e4m3fn[1280,640]{1,0:T(32,128)(4,1)S(1)}) custom-call(s32[40,640]{1,0:T(8,128)S(1)} %bitcast.9, s32[40,640]{1,0:T(8,128)S(1)} %collective-permute-done.2.r2), custom_call_target="tpu_custom_call" | custom-call | flops 100000000 | bytes 5000000 | tf_op jit(solution)/shard_map/pallas_call | solution.py:205
  32.7 1.4 %shard_map.42.paths = f32[1280,640]{1,0:T(8,128)S(1)} custom-call(s32[8,40,640]{2,1,0:T(8,128)S(1)} %all_to_all.10.own, f8e4m3fn[1280,640]{1,0:T(32,128)(4,1)S(1)} %get-tuple-element.7.right), custom_call_target="tpu_custom_call" | custom-call | flops 2097152000 | bytes 5000000 | tf_op jit(solution)/shard_map/pallas_call | solution.py:205
  34.1 0.0 collective-permute-done.1.r1
  34.1 0.1 collective-permute-done.3.r3
  34.3 0.0 collective-permute-done.4.r4
  34.3 0.0 collective-permute-done.oth
  34.3 0.0 copy-start.1
  34.3 6.2 %shard_map.43 = f32[64,8,128]{2,1,0:T(8,128)S(1)} custom-call(s32[8,40,640]{2,1,0:T(8,128)S(1)} %all_to_all.10.own, s32[8,40,640]{2,1,0:T(8,128)S(1)} %collective-permute-done.oth, s32[40,640]{1,0:T(8,128)S(1)} %collective-permute-done.1.r1, s32[40,640]{1,0:T(8,128)S(1)} %collective-permute-done.2.r2, s32[40,640]{1,0:T(8,128)S(1)} %collective-permute-done.3.r3, ...), custom_call_target="tpu_custom_call" | custom-call | flops 8388608000 | bytes 5000000 | tf_op jit(solution)/shard_map/pallas_call | solution.py:205
  40.5 19.6 %all_to_all.11.own = f32[64,8,128]{2,1,0:T(8,128)S(1)} all-to-all(f32[64,8,128]{2,1,0:T(8,128)S(1)} %shard_map.43), channel_id=1, replica_groups={{0,1,2,3,4,5,6,7,16,17,18,19,20,21,22,23,32,33,34,35,36,37,38,39,48,49,..., dimensions={0} | all-to-all | bytes 524288 | tf_op jit(solution)/shard_map/all_to_all | solution.py:243
  60.1 2.1 %collective-permute-start.5 = (f32[64,8,128]{2,1,0:T(8,128)S(1)}, f32[64,8,128]{2,1,0:T(8,128)S(1)}, u32[]{:S(2)}, u32[]{:S(2)}) collective-permute-start(f32[64,8,128]{2,1,0:T(8,128)S(1)} %all_to_all.11.own), channel_id=1, source_target_pairs={{0,8},{8,0},{16,24},{24,16},{32,40},{40,32},{48,56},{56,48},{64,72... | collective-permute-start | bytes 786440 | tf_op jit(solution)/shard_map/ppermute | solution.py:244
  62.1 1.2 %collective-permute-done.5.oth = f32[64,8,128]{2,1,0:T(8,128)S(1)} collective-permute-done((f32[64,8,128]{2,1,0:T(8,128)S(1)}, f32[64,8,128]{2,1,0:T(8,128)S(1)}, u32[]{:S(2)}, u32[]{:S(2)}) %collective-permute-start.5) | collective-permute-done | bytes 262176 | tf_op jit(solution)/shard_map/ppermute | solution.py:244
  63.3 0.0 copy-done.1
  63.3 0.8 %finish.1 = (f32[1,80]{1,0:T(1,128)}, f32[1,1]{1,0:T(1,128)}) custom-call(f32[64,8,128]{2,1,0:T(8,128)S(1)} %all_to_all.11.own, f32[64,8,128]{2,1,0:T(8,128)S(1)} %collective-permute-done.5.oth, s32[1,80]{1,0:T(1,128)S(1)} %bitcast.10), custom_call_target="tpu_custom_call" | custom-call | tf_op jit(solution)/shard_map/finish/pallas_call | solution.py:245
Async XLA Ops:
  19.5 14.7 %collective-permute-start = (s32[8,40,640]{2,1,0:T(8,128)S(1)}, s32[8,40,640]{2,1,0:T(8,128)S(1)}, u32[]{:S(2)}, u32[]{:S(2)}) collective-permute-start(s32[8,40,640]{2,1,0:T(8,128)S(1)} %all_to_all.10.own), channel_id=1, source_target_pairs={{0,8},{8,0},{16,24},{24,16},{32,40},{40,32},{48,56},{56,48},{64,72... | collective-permute-start | bytes 2457608 | tf_op jit(solution)/shard_map/ppermute | solution.py:196
  21.7 9.4 %collective-permute-start.2 = (s32[40,640]{1,0:T(8,128)}, s32[40,640]{1,0:T(8,128)S(1)}, u32[]{:S(2)}, u32[]{:S(2)}) collective-permute-start(s32[40,640]{1,0:T(8,128)} %bitcast.5), channel_id=1, source_target_pairs={{1,0},{2,1},{3,2},{0,3},{5,4},{6,5},{7,6},{4,7},{9,8},{10,9},{11,1... | collective-permute-start | bytes 307208 | tf_op jit(solution)/shard_map/ppermute | solution.py:192
  25.5 8.7 %collective-permute-start.1 = (s32[40,640]{1,0:T(8,128)}, s32[40,640]{1,0:T(8,128)S(1)}, u32[]{:S(2)}, u32[]{:S(2)}) collective-permute-start(s32[40,640]{1,0:T(8,128)} %bitcast.6), channel_id=1, source_target_pairs={{4,0},{5,1},{6,2},{7,3},{1,4},{2,5},{3,6},{0,7},{12,8},{13,9},{14,... | collective-permute-start | bytes 307208 | tf_op jit(solution)/shard_map/ppermute | solution.py:192
  27.8 6.5 %collective-permute-start.3 = (s32[40,640]{1,0:T(8,128)}, s32[40,640]{1,0:T(8,128)S(1)}, u32[]{:S(2)}, u32[]{:S(2)}) collective-permute-start(s32[40,640]{1,0:T(8,128)} %bitcast.7), channel_id=1, source_target_pairs={{5,0},{6,1},{7,2},{4,3},{2,4},{3,5},{0,6},{1,7},{13,8},{14,9},{15,... | collective-permute-start | bytes 307208 | tf_op jit(solution)/shard_map/ppermute | solution.py:192
  28.0 6.3 %collective-permute-start.4 = (s32[40,640]{1,0:T(8,128)}, s32[40,640]{1,0:T(8,128)S(1)}, u32[]{:S(2)}, u32[]{:S(2)}) collective-permute-start(s32[40,640]{1,0:T(8,128)} %bitcast.8), channel_id=1, source_target_pairs={{2,0},{3,1},{0,2},{1,3},{6,4},{7,5},{4,6},{5,7},{10,8},{11,9},{8,1... | collective-permute-start | bytes 307208 | tf_op jit(solution)/shard_map/ppermute | solution.py:192
  31.1 0.9 %copy-start = (s32[640,40]{0,1:T(8,128)S(1)}, s32[640,40]{0,1:T(8,128)}, u32[]{:S(2)}) copy-start(s32[640,40]{0,1:T(8,128)} %param.2) | copy-start | bytes 307204
  34.3 29.0 %copy-start.1 = (s32[80]{0:T(128)S(1)}, s32[80]{0:T(128)}, u32[]{:S(2)}) copy-start(s32[80]{0:T(128)} %param.3) | copy-start | bytes 964
  60.1 3.2 %collective-permute-start.5 = (f32[64,8,128]{2,1,0:T(8,128)S(1)}, f32[64,8,128]{2,1,0:T(8,128)S(1)}, u32[]{:S(2)}, u32[]{:S(2)}) collective-permute-start(f32[64,8,128]{2,1,0:T(8,128)S(1)} %all_to_all.11.own), channel_id=1, source_target_pairs={{0,8},{8,0},{16,24},{24,16},{32,40},{40,32},{48,56},{56,48},{64,72... | collective-permute-start | bytes 786440 | tf_op jit(solution)/shard_map/ppermute | solution.py:244

commit v7 on v6

--- a/solution.py
+++ b/solution.py
@@ -76,21 +76,20 @@
         fill_right(right_next, rows, REST[0], tile, core)
 
 
-def product(left, right, tile):
+def product(left, right, first, count):
     return jnp.dot(
-        left[tile * TILE : tile * TILE + TILE, :],
-        right[...],
-        preferred_element_type=jnp.float32,
+        left[first : first + count, :], right[...], preferred_element_type=jnp.float32
     )
 
 
 def begin_kernel(own, right, paths, left):
     places = places_of(lax.axis_index("col"))
-    fill_left(left, (own,), FIRST[0], 0, places)
-    for tile in range(5):
-        if tile < 4:
-            fill_left(left, (own,), FIRST[0], tile + 1, places)
-        paths[tile * TILE : tile * TILE + TILE, :] = product(left, right, tile)
+    filled = 0
+    for first in range(0, 1280, 640):
+        while filled < 5 and filled * TILE < first + 2 * 640:
+            fill_left(left, (own,), FIRST[0], filled, places)
+            filled += 1
+        paths[first : first + 640, :] = product(left, right, first, 640)
 
 
 def count_kernel(own, oth, r1, r2, r3, r4, right_next, paths, out, la, lb, ra, rb, acc):
@@ -105,24 +104,27 @@
     for tile in range(5):
         fill_left(la, (own, oth), REST[0], tile, places)
     total = jnp.zeros((8, lanes), jnp.float32)
+    size = 640
     for k in range(len(REST)):
         now, later = k % 2, (k + 1) % 2
         known = paths if k == 0 else acc
-        for tile in range(5):
+        factor = right_next if k == 0 else right[now]
+        filled = 0
+        for first in range(0, 1280, size):
+            while k + 1 < len(REST) and filled < 5 and filled * TILE < first + size:
+                fill_left(left[later], (own, oth), REST[k + 1], filled, places)
+                fill_right(right[later], rows, REST[k + 1], filled, core)
+                filled += 1
+            value = known[first : first + size, :] + product(left[now], factor, first, size)
             if k + 1 < len(REST):
-                fill_left(left[later], (own, oth), REST[k + 1], tile, places)
-                fill_right(right[later], rows, REST[k + 1], tile, core)
-            piece = slice(tile * TILE, tile * TILE + TILE)
-            factor = right_next if k == 0 else right[now]
-            value = known[piece, :] + product(left[now], factor, tile)
-            if k + 1 < len(REST):
-                acc[piece, :] = value
+                acc[first : first + size, :] = value
                 continue
-            words = mask[8 * tile : 8 * tile + 8, :]
-            for s in range(8):
+            for chunk in range(first // 32, (first + size) // 32):
+                tile, s = chunk // 8, chunk % 8
+                words = mask[8 * tile : 8 * tile + 8, :]
                 part = 0.0
                 for byte in range(4):
-                    at = s * 32 + byte * 8
+                    at = chunk * 32 - first + byte * 8
                     spot = 8 * byte + s
                     hit = (words & jnp.int32(-(2**31) if spot == 31 else 1 << spot)) != 0
                     part = part + jnp.where(hit, value[at : at + 8, :], 0.0)

time: 64.4 us -> 64 us (level)
  no operation moved by 1% of the time
where the time goes in v7:
time: 64 us; the launch traced here: 63.8 us
  blocking collectives  37.5 us (59%)
  starting transfers between devices  13.7 us (21%)
  Pallas kernels  8.74 us (14%)
  local copies, waits for them, and re-layouts  1.88 us (3%)
  waiting for transfers between devices  1.29 us (2%)
  between operations  0.67 us (1%)
    all_to_all x1, blocking collectives, body(): lax.all_to_all(payload, ALL, 0, 0, axis_index_groups=peers, tiled=True)  19.6 us
    all_to_all x1, blocking collectives, body(): lax.all_to_all(spread(words, 8), 'row', 0, 0, axis_index_groups=cores, ti...  17.9 us
    ppermute x4, starting transfers between devices, body(): lax.ppermute(words, 'col', [(place_of(label_of(c) + t), c) for c in range...  9.41 us
    pallas_call x3, Pallas kernels, call(): pl.pallas_call(kernel, out_shape=out_shape, in_specs=[vmem] * len(operand...  7.92 us
    ppermute x1, starting transfers between devices, body(): oth = lax.ppermute(own, 'row', [(r, r ^ 1) for r in range(16)])  2.19 us
    ppermute x1, starting transfers between devices, body(): across = lax.ppermute(parts, 'row', [(r, r ^ 1) for r in range(16)])  2.07 us
  transfers between devices with their start and end apart: 6, of which 2 were waited for; matrix products, arithmetic and copies ran while one was open for 0% of the time, Pallas kernels for 3%

profile of v7, /device:TPU:1, one launch (start us, length us, event | category | flops | bytes accessed | tf_op | source)
XLA Modules:
  0.0 63.8 jit_solution(4306999218046179663)
XLA Ops:
  0.6 0.9 %broadcast_in_dim.4 = s32[8,40,640]{2,1,0:T(8,128)S(1)} broadcast(s32[40,640]{1,0:T(8,128)} %bitcast.4), dimensions={1,2} | broadcast | bytes 921600 | tf_op jit(solution)/shard_map/broadcast_in_dim | solution.py:13
  1.6 17.9 %all_to_all.10.own = s32[8,40,640]{2,1,0:T(8,128)S(1)} all-to-all(s32[8,40,640]{2,1,0:T(8,128)S(1)} %broadcast_in_dim.4), channel_id=1, replica_groups={{0,16,32,48,64,80,96,112},{8,24,40,56,72,88,104,120},{1,17,33,49,65,81,..., dimensions={0} | all-to-all | bytes 1638400 | tf_op jit(solution)/shard_map/all_to_all | solution.py:188
  19.5 2.2 %collective-permute-start = (s32[8,40,640]{2,1,0:T(8,128)S(1)}, s32[8,40,640]{2,1,0:T(8,128)S(1)}, u32[]{:S(2)}, u32[]{:S(2)}) collective-permute-start(s32[8,40,640]{2,1,0:T(8,128)S(1)} %all_to_all.10.own), channel_id=1, source_target_pairs={{0,8},{8,0},{16,24},{24,16},{32,40},{40,32},{48,56},{56,48},{64,72... | collective-permute-start | bytes 2457608 | tf_op jit(solution)/shard_map/ppermute | solution.py:198
  21.7 3.8 %collective-permute-start.2 = (s32[40,640]{1,0:T(8,128)}, s32[40,640]{1,0:T(8,128)S(1)}, u32[]{:S(2)}, u32[]{:S(2)}) collective-permute-start(s32[40,640]{1,0:T(8,128)} %bitcast.5), channel_id=1, source_target_pairs={{1,0},{2,1},{3,2},{0,3},{5,4},{6,5},{7,6},{4,7},{9,8},{10,9},{11,1... | collective-permute-start | bytes 307208 | tf_op jit(solution)/shard_map/ppermute | solution.py:194
  25.5 2.3 %collective-permute-start.1 = (s32[40,640]{1,0:T(8,128)}, s32[40,640]{1,0:T(8,128)S(1)}, u32[]{:S(2)}, u32[]{:S(2)}) collective-permute-start(s32[40,640]{1,0:T(8,128)} %bitcast.6), channel_id=1, source_target_pairs={{4,0},{5,1},{6,2},{7,3},{1,4},{2,5},{3,6},{0,7},{12,8},{13,9},{14,... | collective-permute-start | bytes 307208 | tf_op jit(solution)/shard_map/ppermute | solution.py:194
  27.8 0.2 collective-permute-start.3
  28.0 3.1 %collective-permute-start.4 = (s32[40,640]{1,0:T(8,128)}, s32[40,640]{1,0:T(8,128)S(1)}, u32[]{:S(2)}, u32[]{:S(2)}) collective-permute-start(s32[40,640]{1,0:T(8,128)} %bitcast.8), channel_id=1, source_target_pairs={{2,0},{3,1},{0,2},{1,3},{6,4},{7,5},{4,6},{5,7},{10,8},{11,9},{8,1... | collective-permute-start | bytes 307208 | tf_op jit(solution)/shard_map/ppermute | solution.py:194
  31.1 0.0 collective-permute-done.2.r2
  31.1 0.0 copy-start
  31.1 0.9 %copy-done = s32[640,40]{0,1:T(8,128)S(1)} copy-done((s32[640,40]{0,1:T(8,128)S(1)}, s32[640,40]{0,1:T(8,128)}, u32[]{:S(2)}) %copy-start) | copy-done | bytes 102424
  32.1 0.7 %shard_map.41 = (f8e4m3fn[1280,640]{1,0:T(32,128)(4,1)S(1)}, f8e4m3fn[1280,640]{1,0:T(32,128)(4,1)S(1)}) custom-call(s32[40,640]{1,0:T(8,128)S(1)} %bitcast.9, s32[40,640]{1,0:T(8,128)S(1)} %collective-permute-done.2.r2), custom_call_target="tpu_custom_call" | custom-call | flops 100000000 | bytes 5000000 | tf_op jit(solution)/shard_map/pallas_call | solution.py:207
  32.7 1.4 %shard_map.42.paths = f32[1280,640]{1,0:T(8,128)S(1)} custom-call(s32[8,40,640]{2,1,0:T(8,128)S(1)} %all_to_all.10.own, f8e4m3fn[1280,640]{1,0:T(32,128)(4,1)S(1)} %get-tuple-element.7.right), custom_call_target="tpu_custom_call" | custom-call | flops 2097152000 | bytes 5000000 | tf_op jit(solution)/shard_map/pallas_call | solution.py:207
  34.1 0.0 collective-permute-done.1.r1
  34.1 0.1 collective-permute-done.3.r3
  34.3 0.0 collective-permute-done.4.r4
  34.3 0.0 collective-permute-done.oth
  34.3 0.0 copy-start.1
  34.3 5.9 %shard_map.43 = f32[64,8,128]{2,1,0:T(8,128)S(1)} custom-call(s32[8,40,640]{2,1,0:T(8,128)S(1)} %all_to_all.10.own, s32[8,40,640]{2,1,0:T(8,128)S(1)} %collective-permute-done.oth, s32[40,640]{1,0:T(8,128)S(1)} %collective-permute-done.1.r1, s32[40,640]{1,0:T(8,128)S(1)} %collective-permute-done.2.r2, s32[40,640]{1,0:T(8,128)S(1)} %collective-permute-done.3.r3, ...), custom_call_target="tpu_custom_call" | custom-call | flops 8388608000 | bytes 5000000 | tf_op jit(solution)/shard_map/pallas_call | solution.py:207
  40.1 19.6 %all_to_all.11.own = f32[64,8,128]{2,1,0:T(8,128)S(1)} all-to-all(f32[64,8,128]{2,1,0:T(8,128)S(1)} %shard_map.43), channel_id=1, replica_groups={{0,1,2,3,4,5,6,7,16,17,18,19,20,21,22,23,32,33,34,35,36,37,38,39,48,49,..., dimensions={0} | all-to-all | bytes 524288 | tf_op jit(solution)/shard_map/all_to_all | solution.py:245
  59.7 2.1 %collective-permute-start.5 = (f32[64,8,128]{2,1,0:T(8,128)S(1)}, f32[64,8,128]{2,1,0:T(8,128)S(1)}, u32[]{:S(2)}, u32[]{:S(2)}) collective-permute-start(f32[64,8,128]{2,1,0:T(8,128)S(1)} %all_to_all.11.own), channel_id=1, source_target_pairs={{0,8},{8,0},{16,24},{24,16},{32,40},{40,32},{48,56},{56,48},{64,72... | collective-permute-start | bytes 786440 | tf_op jit(solution)/shard_map/ppermute | solution.py:246
  61.8 1.2 %collective-permute-done.5.oth = f32[64,8,128]{2,1,0:T(8,128)S(1)} collective-permute-done((f32[64,8,128]{2,1,0:T(8,128)S(1)}, f32[64,8,128]{2,1,0:T(8,128)S(1)}, u32[]{:S(2)}, u32[]{:S(2)}) %collective-permute-start.5) | collective-permute-done | bytes 262176 | tf_op jit(solution)/shard_map/ppermute | solution.py:246
  63.0 0.0 copy-done.1
  63.0 0.8 %finish.1 = (f32[1,80]{1,0:T(1,128)}, f32[1,1]{1,0:T(1,128)}) custom-call(f32[64,8,128]{2,1,0:T(8,128)S(1)} %all_to_all.11.own, f32[64,8,128]{2,1,0:T(8,128)S(1)} %collective-permute-done.5.oth, s32[1,80]{1,0:T(1,128)S(1)} %bitcast.10), custom_call_target="tpu_custom_call" | custom-call | tf_op jit(solution)/shard_map/finish/pallas_call | solution.py:247
Async XLA Ops:
  19.5 14.7 %collective-permute-start = (s32[8,40,640]{2,1,0:T(8,128)S(1)}, s32[8,40,640]{2,1,0:T(8,128)S(1)}, u32[]{:S(2)}, u32[]{:S(2)}) collective-permute-start(s32[8,40,640]{2,1,0:T(8,128)S(1)} %all_to_all.10.own), channel_id=1, source_target_pairs={{0,8},{8,0},{16,24},{24,16},{32,40},{40,32},{48,56},{56,48},{64,72... | collective-permute-start | bytes 2457608 | tf_op jit(solution)/shard_map/ppermute | solution.py:198
  21.7 9.4 %collective-permute-start.2 = (s32[40,640]{1,0:T(8,128)}, s32[40,640]{1,0:T(8,128)S(1)}, u32[]{:S(2)}, u32[]{:S(2)}) collective-permute-start(s32[40,640]{1,0:T(8,128)} %bitcast.5), channel_id=1, source_target_pairs={{1,0},{2,1},{3,2},{0,3},{5,4},{6,5},{7,6},{4,7},{9,8},{10,9},{11,1... | collective-permute-start | bytes 307208 | tf_op jit(solution)/shard_map/ppermute | solution.py:194
  25.5 8.7 %collective-permute-start.1 = (s32[40,640]{1,0:T(8,128)}, s32[40,640]{1,0:T(8,128)S(1)}, u32[]{:S(2)}, u32[]{:S(2)}) collective-permute-start(s32[40,640]{1,0:T(8,128)} %bitcast.6), channel_id=1, source_target_pairs={{4,0},{5,1},{6,2},{7,3},{1,4},{2,5},{3,6},{0,7},{12,8},{13,9},{14,... | collective-permute-start | bytes 307208 | tf_op jit(solution)/shard_map/ppermute | solution.py:194
  27.8 6.5 %collective-permute-start.3 = (s32[40,640]{1,0:T(8,128)}, s32[40,640]{1,0:T(8,128)S(1)}, u32[]{:S(2)}, u32[]{:S(2)}) collective-permute-start(s32[40,640]{1,0:T(8,128)} %bitcast.7), channel_id=1, source_target_pairs={{5,0},{6,1},{7,2},{4,3},{2,4},{3,5},{0,6},{1,7},{13,8},{14,9},{15,... | collective-permute-start | bytes 307208 | tf_op jit(solution)/shard_map/ppermute | solution.py:194
  28.0 6.3 %collective-permute-start.4 = (s32[40,640]{1,0:T(8,128)}, s32[40,640]{1,0:T(8,128)S(1)}, u32[]{:S(2)}, u32[]{:S(2)}) collective-permute-start(s32[40,640]{1,0:T(8,128)} %bitcast.8), channel_id=1, source_target_pairs={{2,0},{3,1},{0,2},{1,3},{6,4},{7,5},{4,6},{5,7},{10,8},{11,9},{8,1... | collective-permute-start | bytes 307208 | tf_op jit(solution)/shard_map/ppermute | solution.py:194
  31.1 0.9 %copy-start = (s32[640,40]{0,1:T(8,128)S(1)}, s32[640,40]{0,1:T(8,128)}, u32[]{:S(2)}) copy-start(s32[640,40]{0,1:T(8,128)} %param.2) | copy-start | bytes 307204
  34.3 28.7 %copy-start.1 = (s32[80]{0:T(128)S(1)}, s32[80]{0:T(128)}, u32[]{:S(2)}) copy-start(s32[80]{0:T(128)} %param.3) | copy-start | bytes 964
  59.7 3.2 %collective-permute-start.5 = (f32[64,8,128]{2,1,0:T(8,128)S(1)}, f32[64,8,128]{2,1,0:T(8,128)S(1)}, u32[]{:S(2)}, u32[]{:S(2)}) collective-permute-start(f32[64,8,128]{2,1,0:T(8,128)S(1)} %all_to_all.11.own), channel_id=1, source_target_pairs={{0,8},{8,0},{16,24},{24,16},{32,40},{40,32},{48,56},{56,48},{64,72... | collective-permute-start | bytes 786440 | tf_op jit(solution)/shard_map/ppermute | solution.py:246

commit v8 on v7

--- a/solution.py
+++ b/solution.py
@@ -27,6 +27,7 @@
 FIRST = (((0, 0), (0, 2)),)
 REST = (((1, 0), (1, 2)), ((0, 4), (1, 4)), ((0, 1), (1, 1)), ((0, 3), (1, 3)))
 WEIGHTS = (1, 2, 2, 2, 1)
+PART = 384
 
 
 TILE = 256
@@ -37,8 +38,9 @@
     for w in range(8 * tile, 8 * tile + 8):
         side, t = step[w // half]
         base = half * (core if side == 0 else 1 - core) + w % half
-        target[w * 32 : w * 32 + 32, :] = weighted(
-            rows[t][pl.ds(base, 1), :], WEIGHTS[t], target.dtype
+        row = rows[t][pl.ds(base, 1), :]
+        target[w * 32 : w * 32 + 32, : row.shape[1]] = weighted(
+            row, WEIGHTS[t], target.dtype
         )
 
 
@@ -76,10 +78,26 @@
         fill_right(right_next, rows, REST[0], tile, core)
 
 
-def product(left, right, first, count):
+def product(left, right, first, count, lanes=640):
     return jnp.dot(
-        left[first : first + count, :], right[...], preferred_element_type=jnp.float32
-    )
+        left[first : first + count, :],
+        right[:, :lanes],
+        preferred_element_type=jnp.float32,
+    )
+
+
+def masked_sum(total, value, first, words_of):
+    for chunk in range(first // 32, (first + value.shape[0]) // 32):
+        tile, s = chunk // 8, chunk % 8
+        words = words_of(tile)
+        part = 0.0
+        for byte in range(4):
+            at = chunk * 32 - first + byte * 8
+            spot = 8 * byte + s
+            hit = (words & jnp.int32(-(2**31) if spot == 31 else 1 << spot)) != 0
+            part = part + jnp.where(hit, value[at : at + 8, :], 0.0)
+        total = total + part * (-(2.0**-7) if s == 7 else 2.0**-s)
+    return total
 
 
 def begin_kernel(own, right, paths, left):
@@ -103,33 +121,48 @@
     left, right = (la, lb), (ra, rb)
     for tile in range(5):
         fill_left(la, (own, oth), REST[0], tile, places)
+    low = label_of(col) < 4
+    part_lane = lax.broadcasted_iota(jnp.int32, (8, PART), 1)
+
+    def all_words(tile):
+        return mask[8 * tile : 8 * tile + 8, :]
+
+    def part_words(tile):
+        words = all_words(tile)
+        picked = jnp.where(low, words[:, :PART], words[:, lanes - PART :])
+        return jnp.where(low | (part_lane >= 2 * PART - lanes), picked, 0)
+
     total = jnp.zeros((8, lanes), jnp.float32)
+    shared = jnp.zeros((8, PART), jnp.float32)
     size = 640
-    for k in range(len(REST)):
+    for k, step in enumerate(REST):
         now, later = k % 2, (k + 1) % 2
         known = paths if k == 0 else acc
         factor = right_next if k == 0 else right[now]
+        opposite = step[0][1] == 4
         filled = 0
         for first in range(0, 1280, size):
             while k + 1 < len(REST) and filled < 5 and filled * TILE < first + size:
                 fill_left(left[later], (own, oth), REST[k + 1], filled, places)
                 fill_right(right[later], rows, REST[k + 1], filled, core)
                 filled += 1
+            if opposite:
+                value = product(left[now], factor, first, size, PART)
+                shared = masked_sum(shared, value, first, part_words)
+                continue
             value = known[first : first + size, :] + product(left[now], factor, first, size)
             if k + 1 < len(REST):
                 acc[first : first + size, :] = value
-                continue
-            for chunk in range(first // 32, (first + size) // 32):
-                tile, s = chunk // 8, chunk % 8
-                words = mask[8 * tile : 8 * tile + 8, :]
-                part = 0.0
-                for byte in range(4):
-                    at = chunk * 32 - first + byte * 8
-                    spot = 8 * byte + s
-                    hit = (words & jnp.int32(-(2**31) if spot == 31 else 1 << spot)) != 0
-                    part = part + jnp.where(hit, value[at : at + 8, :], 0.0)
-                total = total + part * (-(2.0**-7) if s == 7 else 2.0**-s)
+            else:
+                total = masked_sum(total, value, first, all_words)
     closed = jnp.sum(total, axis=0, keepdims=True)
+    halves = 2.0 * jnp.sum(shared, axis=0, keepdims=True)
+    above = jnp.zeros((1, lanes - PART), jnp.float32)
+    closed = closed + jnp.where(
+        low,
+        jnp.concatenate([halves, above], axis=1),
+        jnp.concatenate([above, halves], axis=1),
+    )
     links = sum(lax.population_count(rows[t][...]) for t in range(4))
     degree = jnp.sum(links, axis=0, keepdims=True).astype(jnp.float32)
     part = label_of(col) % 4
@@ -189,10 +222,13 @@
         spread(words, 8), "row", 0, 0, axis_index_groups=cores, tiled=True
     )
     rows = [words]
+    start = jnp.where(label_of(lax.axis_index("col")) < 4, words.shape[1] - PART, 0)
+    opposite = lax.dynamic_slice_in_dim(words, start, PART, axis=1)
     for t in range(1, WINDOW):
+        sent = words if t < 4 else opposite
         rows.append(
             lax.ppermute(
-                words, "col", [(place_of(label_of(c) + t), c) for c in range(8)]
+                sent, "col", [(place_of(label_of(c) + t), c) for c in range(8)]
             )
         )
     oth = lax.ppermute(own, "row", [(r, r ^ 1) for r in range(16)])

time: 64 us -> 63 us (0.984)
  blocking collectives: 37.5 us -> 35.9 us
  local copies, waits for them, and re-layouts: 1.88 us -> 2.72 us
    all_to_all x1, blocking collectives: 19.6 us -> 18 us  [body(): lax.all_to_all(payload, ALL, 0, 0, axis_index_groups=peers, tiled=True)]
    dynamic_slice x0 -> x1, local copies, waits for them, and re-layouts: none -> 0.87 us  [body(): opposite = lax.dynamic_slice_in_dim(words, start, PART, axis=1)]
  transfers between devices with their start and end apart: 6 -> 6, of which waited for: 2 -> 1; matrix products, arithmetic and copies ran while one was open for 0% -> 1% of each run, Pallas kernels for 3% -> 3%
where the time goes in v8:
time: 63 us; the launch traced here: 62.7 us
  blocking collectives  35.9 us (57%)
  starting transfers between devices  13.7 us (22%)
  Pallas kernels  8.5 us (13%)
  local copies, waits for them, and re-layouts  2.72 us (4%)
  waiting for transfers between devices  1.18 us (2%)
  between operations  0.7 us (1%)
    all_to_all x1, blocking collectives, body(): lax.all_to_all(payload, ALL, 0, 0, axis_index_groups=peers, tiled=True)  18 us
    all_to_all x1, blocking collectives, body(): lax.all_to_all(spread(words, 8), 'row', 0, 0, axis_index_groups=cores, ti...  17.9 us
    ppermute x4, starting transfers between devices, body(): lax.ppermute(sent, 'col', [(place_of(label_of(c) + t), c) for c in range(...  9.41 us
    pallas_call x3, Pallas kernels, call(): pl.pallas_call(kernel, out_shape=out_shape, in_specs=[vmem] * len(operand...  7.68 us
    ppermute x1, starting transfers between devices, body(): oth = lax.ppermute(own, 'row', [(r, r ^ 1) for r in range(16)])  2.19 us
    ppermute x1, starting transfers between devices, body(): across = lax.ppermute(parts, 'row', [(r, r ^ 1) for r in range(16)])  2.07 us
  transfers between devices with their start and end apart: 6, of which 1 were waited for; matrix products, arithmetic and copies ran while one was open for 1% of the time, Pallas kernels for 3%

profile of v8, /device:TPU:1, one launch (start us, length us, event | category | flops | bytes accessed | tf_op | source)
XLA Modules:
  0.0 62.7 jit_solution(11045034623325076002)
XLA Ops:
  0.6 0.9 %broadcast_in_dim.4 = s32[8,40,640]{2,1,0:T(8,128)S(1)} broadcast(s32[40,640]{1,0:T(8,128)} %bitcast.6), dimensions={1,2} | broadcast | bytes 921600 | tf_op jit(solution)/shard_map/broadcast_in_dim | solution.py:13
  1.6 17.9 %all_to_all.10.own = s32[8,40,640]{2,1,0:T(8,128)S(1)} all-to-all(s32[8,40,640]{2,1,0:T(8,128)S(1)} %broadcast_in_dim.4), channel_id=1, replica_groups={{0,16,32,48,64,80,96,112},{8,24,40,56,72,88,104,120},{1,17,33,49,65,81,..., dimensions={0} | all-to-all | bytes 1638400 | tf_op jit(solution)/shard_map/all_to_all | solution.py:221
  19.5 2.2 %collective-permute-start = (s32[8,40,640]{2,1,0:T(8,128)S(1)}, s32[8,40,640]{2,1,0:T(8,128)S(1)}, u32[]{:S(2)}, u32[]{:S(2)}) collective-permute-start(s32[8,40,640]{2,1,0:T(8,128)S(1)} %all_to_all.10.own), channel_id=1, source_target_pairs={{0,8},{8,0},{16,24},{24,16},{32,40},{40,32},{48,56},{56,48},{64,72... | collective-permute-start | bytes 2457608 | tf_op jit(solution)/shard_map/ppermute | solution.py:234
  21.7 3.8 %collective-permute-start.2 = (s32[40,640]{1,0:T(8,128)}, s32[40,640]{1,0:T(8,128)S(1)}, u32[]{:S(2)}, u32[]{:S(2)}) collective-permute-start(s32[40,640]{1,0:T(8,128)} %bitcast.7), channel_id=1, source_target_pairs={{1,0},{2,1},{3,2},{0,3},{5,4},{6,5},{7,6},{4,7},{9,8},{10,9},{11,1... | collective-permute-start | bytes 307208 | tf_op jit(solution)/shard_map/ppermute | solution.py:230
  25.5 2.3 %collective-permute-start.1 = (s32[40,640]{1,0:T(8,128)}, s32[40,640]{1,0:T(8,128)S(1)}, u32[]{:S(2)}, u32[]{:S(2)}) collective-permute-start(s32[40,640]{1,0:T(8,128)} %bitcast.8), channel_id=1, source_target_pairs={{4,0},{5,1},{6,2},{7,3},{1,4},{2,5},{3,6},{0,7},{12,8},{13,9},{14,... | collective-permute-start | bytes 307208 | tf_op jit(solution)/shard_map/ppermute | solution.py:230
  27.8 0.2 collective-permute-start.3
  28.0 0.9 %dynamic-slice_bitcast_fusion = s32[40,384]{1,0:T(8,128)S(1)} fusion(s32[640,40]{0,1:T(8,128)} %param.2, s32[]{:T(128)S(6)} %select_n.18), kind=kLoop, calls=%fused_computation | loop fusion | bytes 122884 | tf_op jit(solution)/shard_map/dynamic_slice | solution.py:226
  28.9 3.1 %collective-permute-start.4 = (s32[40,384]{1,0:T(8,128)S(1)}, s32[40,384]{1,0:T(8,128)S(1)}, u32[]{:S(2)}, u32[]{:S(2)}) collective-permute-start(s32[40,384]{1,0:T(8,128)S(1)} %dynamic-slice_bitcast_fusion), channel_id=1, source_target_pairs={{2,0},{3,1},{0,2},{1,3},{6,4},{7,5},{4,6},{5,7},{10,8},{11,9},{8,1... | collective-permute-start | bytes 184328 | tf_op jit(solution)/shard_map/ppermute | solution.py:230
  32.0 0.0 collective-permute-done.2.r2
  32.0 0.0 copy-start
  32.0 0.9 %copy-done = s32[640,40]{0,1:T(8,128)S(1)} copy-done((s32[640,40]{0,1:T(8,128)S(1)}, s32[640,40]{0,1:T(8,128)}, u32[]{:S(2)}) %copy-start) | copy-done | bytes 102424
  32.9 0.7 %shard_map.41 = (f8e4m3fn[1280,640]{1,0:T(32,128)(4,1)S(1)}, f8e4m3fn[1280,640]{1,0:T(32,128)(4,1)S(1)}) custom-call(s32[40,640]{1,0:T(8,128)S(1)} %bitcast.10, s32[40,640]{1,0:T(8,128)S(1)} %collective-permute-done.2.r2), custom_call_target="tpu_custom_call" | custom-call | flops 100000000 | bytes 5000000 | tf_op jit(solution)/shard_map/pallas_call | solution.py:243
  33.6 1.4 %shard_map.42.paths = f32[1280,640]{1,0:T(8,128)S(1)} custom-call(s32[8,40,640]{2,1,0:T(8,128)S(1)} %all_to_all.10.own, f8e4m3fn[1280,640]{1,0:T(32,128)(4,1)S(1)} %get-tuple-element.7.right), custom_call_target="tpu_custom_call" | custom-call | flops 2097152000 | bytes 5000000 | tf_op jit(solution)/shard_map/pallas_call | solution.py:243
  35.0 0.0 collective-permute-done.4.r4
  35.0 0.0 collective-permute-done.1.r1
  35.0 0.0 collective-permute-done.3.r3
  35.0 0.0 collective-permute-done.oth
  35.0 0.0 copy-start.1
  35.0 5.6 %shard_map.43 = f32[64,8,128]{2,1,0:T(8,128)S(1)} custom-call(s32[8,40,640]{2,1,0:T(8,128)S(1)} %all_to_all.10.own, s32[8,40,640]{2,1,0:T(8,128)S(1)} %collective-permute-done.oth, s32[40,640]{1,0:T(8,128)S(1)} %collective-permute-done.1.r1, s32[40,640]{1,0:T(8,128)S(1)} %collective-permute-done.2.r2, s32[40,640]{1,0:T(8,128)S(1)} %collective-permute-done.3.r3, ...), custom_call_target="tpu_custom_call" | custom-call | flops 8388608000 | bytes 5000000 | tf_op jit(solution)/shard_map/pallas_call | solution.py:243
  40.6 18.0 %all_to_all.11.own = f32[64,8,128]{2,1,0:T(8,128)S(1)} all-to-all(f32[64,8,128]{2,1,0:T(8,128)S(1)} %shard_map.43), channel_id=1, replica_groups={{0,1,2,3,4,5,6,7,16,17,18,19,20,21,22,23,32,33,34,35,36,37,38,39,48,49,..., dimensions={0} | all-to-all | bytes 524288 | tf_op jit(solution)/shard_map/all_to_all | solution.py:281
  58.6 2.1 %collective-permute-start.5 = (f32[64,8,128]{2,1,0:T(8,128)S(1)}, f32[64,8,128]{2,1,0:T(8,128)S(1)}, u32[]{:S(2)}, u32[]{:S(2)}) collective-permute-start(f32[64,8,128]{2,1,0:T(8,128)S(1)} %all_to_all.11.own), channel_id=1, source_target_pairs={{0,8},{8,0},{16,24},{24,16},{32,40},{40,32},{48,56},{56,48},{64,72... | collective-permute-start | bytes 786440 | tf_op jit(solution)/shard_map/ppermute | solution.py:282
  60.7 1.2 %collective-permute-done.5.oth = f32[64,8,128]{2,1,0:T(8,128)S(1)} collective-permute-done((f32[64,8,128]{2,1,0:T(8,128)S(1)}, f32[64,8,128]{2,1,0:T(8,128)S(1)}, u32[]{:S(2)}, u32[]{:S(2)}) %collective-permute-start.5) | collective-permute-done | bytes 262176 | tf_op jit(solution)/shard_map/ppermute | solution.py:282
  61.9 0.0 copy-done.1
  61.9 0.8 %finish.1 = (f32[1,80]{1,0:T(1,128)}, f32[1,1]{1,0:T(1,128)}) custom-call(f32[64,8,128]{2,1,0:T(8,128)S(1)} %all_to_all.11.own, f32[64,8,128]{2,1,0:T(8,128)S(1)} %collective-permute-done.5.oth, s32[1,80]{1,0:T(1,128)S(1)} %bitcast.11), custom_call_target="tpu_custom_call" | custom-call | tf_op jit(solution)/shard_map/finish/pallas_call | solution.py:283
Async XLA Ops:
  19.5 15.5 %collective-permute-start = (s32[8,40,640]{2,1,0:T(8,128)S(1)}, s32[8,40,640]{2,1,0:T(8,128)S(1)}, u32[]{:S(2)}, u32[]{:S(2)}) collective-permute-start(s32[8,40,640]{2,1,0:T(8,128)S(1)} %all_to_all.10.own), channel_id=1, source_target_pairs={{0,8},{8,0},{16,24},{24,16},{32,40},{40,32},{48,56},{56,48},{64,72... | collective-permute-start | bytes 2457608 | tf_op jit(solution)/shard_map/ppermute | solution.py:234
  21.7 10.3 %collective-permute-start.2 = (s32[40,640]{1,0:T(8,128)}, s32[40,640]{1,0:T(8,128)S(1)}, u32[]{:S(2)}, u32[]{:S(2)}) collective-permute-start(s32[40,640]{1,0:T(8,128)} %bitcast.7), channel_id=1, source_target_pairs={{1,0},{2,1},{3,2},{0,3},{5,4},{6,5},{7,6},{4,7},{9,8},{10,9},{11,1... | collective-permute-start | bytes 307208 | tf_op jit(solution)/shard_map/ppermute | solution.py:230
  25.5 9.5 %collective-permute-start.1 = (s32[40,640]{1,0:T(8,128)}, s32[40,640]{1,0:T(8,128)S(1)}, u32[]{:S(2)}, u32[]{:S(2)}) collective-permute-start(s32[40,640]{1,0:T(8,128)} %bitcast.8), channel_id=1, source_target_pairs={{4,0},{5,1},{6,2},{7,3},{1,4},{2,5},{3,6},{0,7},{12,8},{13,9},{14,... | collective-permute-start | bytes 307208 | tf_op jit(solution)/shard_map/ppermute | solution.py:230
  27.8 7.2 %collective-permute-start.3 = (s32[40,640]{1,0:T(8,128)}, s32[40,640]{1,0:T(8,128)S(1)}, u32[]{:S(2)}, u32[]{:S(2)}) collective-permute-start(s32[40,640]{1,0:T(8,128)} %bitcast.9), channel_id=1, source_target_pairs={{5,0},{6,1},{7,2},{4,3},{2,4},{3,5},{0,6},{1,7},{13,8},{14,9},{15,... | collective-permute-start | bytes 307208 | tf_op jit(solution)/shard_map/ppermute | solution.py:230
  28.9 6.1 %collective-permute-start.4 = (s32[40,384]{1,0:T(8,128)S(1)}, s32[40,384]{1,0:T(8,128)S(1)}, u32[]{:S(2)}, u32[]{:S(2)}) collective-permute-start(s32[40,384]{1,0:T(8,128)S(1)} %dynamic-slice_bitcast_fusion), channel_id=1, source_target_pairs={{2,0},{3,1},{0,2},{1,3},{6,4},{7,5},{4,6},{5,7},{10,8},{11,9},{8,1... | collective-permute-start | bytes 184328 | tf_op jit(solution)/shard_map/ppermute | solution.py:230
  32.0 0.9 %copy-start = (s32[640,40]{0,1:T(8,128)S(1)}, s32[640,40]{0,1:T(8,128)}, u32[]{:S(2)}) copy-start(s32[640,40]{0,1:T(8,128)} %param.2) | copy-start | bytes 307204
  35.0 26.9 %copy-start.1 = (s32[80]{0:T(128)S(1)}, s32[80]{0:T(128)}, u32[]{:S(2)}) copy-start(s32[80]{0:T(128)} %param.3) | copy-start | bytes 964
  58.6 3.2 %collective-permute-start.5 = (f32[64,8,128]{2,1,0:T(8,128)S(1)}, f32[64,8,128]{2,1,0:T(8,128)S(1)}, u32[]{:S(2)}, u32[]{:S(2)}) collective-permute-start(f32[64,8,128]{2,1,0:T(8,128)S(1)} %all_to_all.11.own), channel_id=1, source_target_pairs={{0,8},{8,0},{16,24},{24,16},{32,40},{40,32},{48,56},{56,48},{64,72... | collective-permute-start | bytes 786440 | tf_op jit(solution)/shard_map/ppermute | solution.py:282
